TPU v7x, 64 devices: a 2x2x8 block of a 4x4x8 slice. The times are simulated.
64 devices in a mesh: dp: 4 (over x, y), tp: 16 (over z, core).
Axes of the slice: x: 2, y: 2, z: 8, core: 2. Of those that a mesh axis runs over, the one named last changes fastest.
The devices are a block of a 4x4x8 slice.
Arguments:
- q_hidden: bfloat16 [1024, 32, 1024], P(('dp', 'tp')), parts along dimension 0
- d_hidden: bfloat16 [128, 128, 1024], P(('dp', 'tp')), parts along dimension 0
- q_mask: int32 [1024, 32], P(('dp', 'tp')), parts along dimension 0
- d_mask: int32 [128, 128], P(('dp', 'tp')), parts along dimension 0
- positive: int32 [1024], P(('dp', 'tp')), parts along dimension 0
- w_head: bfloat16 [1024, 32768], P(None, 'tp')
- b_head: float32 [32768], P('tp')
Outputs:
- output 1: float32 [4], P('dp'), parts along dimension 0
- output 2: bfloat16 [4096, 32768], P('dp', 'tp'), parts along dimension 0
- output 3: float32 [131072], P(('dp', 'tp')), parts along dimension 0
- output 4: bfloat16 [1024, 32, 1024], P(('dp', 'tp')), parts along dimension 0
- output 5: bfloat16 [128, 128, 1024], P(('dp', 'tp')), parts along dimension 0
There are 4 independent parts. A program takes and returns all parts, laid end to end along the dimension named above; an argument that names none is the same for every part.
All inputs are finite; a program needn't handle non-finite values.
Results may differ from a plain program's by a relative error of at most 0.0141936.
Values are sent between devices in bfloat16 or wider.
A program may use at most 768 MiB of HBM per device.

v0:
```python
import math
import jax
import jax.numpy as jnp
from jax import lax
from jax.sharding import PartitionSpec as P


def solution(mesh):
    n_group = mesh.shape['tp']
    highest = lax.Precision.HIGHEST
    row_spec = P(('dp', 'tp'))
    mask_spec = P(('dp', 'tp'), None)
    hid_spec = P(('dp', 'tp'), None, None)
    contract_first = (((0,), (0,)), ((), ()))
    contract_last = (((1,), (1,)), ((), ()))

    def head_logits(gathered, w_head, b_head):
        return jnp.einsum('pld,dv->plv', gathered, w_head, preferred_element_type=jnp.float32) + b_head

    def side_reps(hidden, mask_all, w_head, b_head):
        def one_row(row_in):
            hid_row, mask_rows = row_in
            gathered = lax.all_gather(hid_row, 'tp')
            logits = head_logits(gathered, w_head, b_head)
            active = jnp.log1p(jnp.maximum(logits, 0.0)) * mask_rows[:, :, None].astype(jnp.float32)
            return jnp.sum(active, axis=1)
        row_reps = lax.map(one_row, (hidden, jnp.swapaxes(mask_all, 0, 1)))
        return jnp.swapaxes(row_reps, 0, 1).reshape((-1, row_reps.shape[-1]))

    def side_grads(hidden, mask_all, grad_rep, w_head, b_head, acc_init):
        grad_rows = jnp.swapaxes(grad_rep.reshape((n_group, hidden.shape[0], -1)), 0, 1)

        def one_row(acc_pair, row_in):
            acc_w, acc_b = acc_pair
            hid_row, mask_rows, grad_row = row_in
            gathered = lax.all_gather(hid_row, 'tp')
            logits = head_logits(gathered, w_head, b_head)
            relu_slope = jnp.where(logits > 0.0, 1.0 / (1.0 + jnp.maximum(logits, 0.0)), 0.0)
            grad_logits = grad_row[:, None, :] * relu_slope * mask_rows[:, :, None].astype(jnp.float32)
            grad_low = grad_logits.astype(jnp.bfloat16)
            acc_w = acc_w + jnp.einsum('pld,plv->dv', gathered, grad_low, preferred_element_type=jnp.float32)
            acc_b = acc_b + jnp.sum(grad_logits, axis=(0, 1))
            part_hid = jnp.einsum('plv,dv->pld', grad_low, w_head, preferred_element_type=jnp.float32).astype(jnp.bfloat16)
            own_hid = lax.psum_scatter(part_hid, 'tp', scatter_dimension=0, tiled=True)
            return (acc_w, acc_b), own_hid[0]
        return lax.scan(one_row, acc_init, (hidden, jnp.swapaxes(mask_all, 0, 1), grad_rows))

    def local_step(q_hidden, d_hidden, q_mask, d_mask, positive, w_head, b_head):
        hidden_size, vocab_loc = w_head.shape
        vocab_size = vocab_loc * n_group
        q_len = q_hidden.shape[1]
        d_len = d_hidden.shape[1]
        q_batch = q_hidden.shape[0] * n_group
        d_batch = d_hidden.shape[0] * n_group
        value_a11 = q_len * math.sqrt(vocab_size * d_len) / 16.0
        lam_q = 4.0 / (vocab_size * q_len * q_len)
        lam_d = 4.0 / (vocab_size * d_len * d_len)
        q_masks = lax.all_gather(q_mask, 'tp')
        d_masks = lax.all_gather(d_mask, 'tp')
        q_rep = side_reps(q_hidden, q_masks, w_head, b_head)
        d_rep = side_reps(d_hidden, d_masks, w_head, b_head)
        q_mean = jnp.mean(q_rep, axis=0)
        d_mean = jnp.mean(d_rep, axis=0)
        score_part = lax.dot_general(q_rep, d_rep, contract_last, precision=highest, preferred_element_type=jnp.float32)
        reg_part = jnp.stack([jnp.sum(q_mean * q_mean), jnp.sum(d_mean * d_mean)])
        score_sum, reg_sum = lax.psum((score_part, reg_part), 'tp')
        scores = score_sum / value_a11
        pos_all = lax.all_gather(positive, 'tp', tiled=True)
        target = (pos_all[:, None] == jnp.arange(d_batch)[None, :]).astype(jnp.float32)
        log_norm = jax.nn.logsumexp(scores, axis=1)
        loss_val = (jnp.mean(log_norm - jnp.sum(scores * target, axis=1))
                    + lam_q * reg_sum[0] + lam_d * reg_sum[1])
        grad_scores = (jnp.exp(scores - log_norm[:, None]) - target) / (q_batch * value_a11)
        grad_q = (jnp.dot(grad_scores, d_rep, precision=highest, preferred_element_type=jnp.float32)
                  + (2.0 * lam_q / q_batch) * q_mean)
        grad_d = (lax.dot_general(grad_scores, q_rep, contract_first, precision=highest, preferred_element_type=jnp.float32)
                  + (2.0 * lam_d / d_batch) * d_mean)
        acc_init = (jnp.zeros((hidden_size, vocab_loc), jnp.float32), jnp.zeros((vocab_loc,), jnp.float32))
        acc_mid, grad_qh = side_grads(q_hidden, q_masks, grad_q, w_head, b_head, acc_init)
        (acc_w, acc_b), grad_dh = side_grads(d_hidden, d_masks, grad_d, w_head, b_head, acc_mid)
        return jnp.reshape(loss_val, (1,)), acc_w.astype(jnp.bfloat16), acc_b, grad_qh, grad_dh

    return jax.shard_map(local_step, mesh=mesh,
                         in_specs=(hid_spec, hid_spec, mask_spec, mask_spec, row_spec, P(None, 'tp'), P('tp')),
                         out_specs=(P('dp'), P('dp', 'tp'), row_spec, hid_spec, hid_spec),
                         check_vma=False)
```

profile of v0, /device:TPU:21, one launch (start us, length us, event | category | flops | bytes accessed | tf_op | source)
XLA Modules:
  0.0 2882.5 jit_solution(2798557240771644409)
XLA Ops:
  30.3 697.2 %while.49 = (s32[]{:T(128)}, f32[16,16,2048]{2,1,0:T(8,128)}, bf16[16,32,1024]{2,1,0:T(8,128)(2,1)}, bf16[1024,2048]{1,0:T(8,128)(2,1)}, f32[2048]{0:T(1024)}, /*index=5*/s32[16,16,32]{2,1,0:T(8,128)S(1)}, s32[]{:T(128)}) while((s32[]{:T(128)}, f32[16,16,2048]{2,1,0:T(8,128)}, bf16[16,32,1024]{2,1,0:T(8,128)(2,1)}, ...), condition=%wide.region_2.3_spmd, body=%wide.region_0.2_spmd.sunk | while | flops 2151645696 | bytes 9123977 | solution.py:27
  746.3 116.2 %while.50 = (s32[]{:T(128)}, f32[2,16,2048]{2,1,0:T(8,128)S(1)}, bf16[2,128,1024]{2,1,0:T(8,128)(2,1)S(1)}, bf16[1024,2048]{1,0:T(8,128)(2,1)}, f32[2048]{0:T(1024)S(1)}, /*index=5*/s32[2,16,128]{2,1,0:T(8,128)S(1)}, s32[]{:T(128)}) while((s32[]{:T(128)}, f32[2,16,2048]{2,1,0:T(8,128)S(1)}, bf16[2,128,1024]{2,1,0:T(8,128)(2,1)S(1)}, ...), condition=%wide.region_5.6_spmd, body=%wide.region_3.5_spmd.sunk | while | flops 8606681088 | bytes 22708360 | solution.py:27
  747.2 40.2 %all-gather.10.cloned.1.call-done = bf16[16,128,1024]{2,1,0:T(8,128)(2,1)} async-done(((bf16[1,128,1024]{2,1,0:T(8,128)(2,1)}), bf16[16,128,1024]{2,1,0:T(8,128)(2,1)}) %all-gather.10.cloned.1.call-update) | async-done | bytes 4194320 | tf_op jit(solution)/shard_map/while/body/eval_jaxpr/all_gather | solution.py:23
  806.0 38.8 %all-gather.10.cloned.1.call-done = bf16[16,128,1024]{2,1,0:T(8,128)(2,1)} async-done(((bf16[1,128,1024]{2,1,0:T(8,128)(2,1)}), bf16[16,128,1024]{2,1,0:T(8,128)(2,1)}) %all-gather.10.cloned.1.call-update) | async-done | bytes 4194320 | tf_op jit(solution)/shard_map/while/body/eval_jaxpr/all_gather | solution.py:23
  869.7 44.3 %all-reduce.1 = (f32[256,32]{0,1:T(8,128)S(1)}, f32[2]{0:T(128)S(1)}) all-reduce(f32[256,32]{0,1:T(8,128)S(1)} %fusion.42, f32[2]{0:T(128)S(1)} %pad_maximum_fusion), channel_id=1, replica_groups=mesh['dp'=4,'tp'=16] {'tp'}, use_global_device_ids=true, to_apply=%region_6.7 | all-reduce | flops 8194 | bytes 65552 | tf_op jit(solution)/shard_map/psum | solution.py:66
  934.5 1667.8 %while.52 = (s32[]{:T(128)}, f32[1024,2048]{1,0:T(8,128)}, f32[2048]{0:T(1024)S(1)}, bf16[16,32,1024]{2,1,0:T(8,128)(2,1)}, bf16[16,32,1024]{2,1,0:T(8,128)(2,1)...) while((s32[]{:T(128)}, f32[1024,2048]{1,0:T(8,128)}, ...), condition=%wide.region_19.20_spmd.clone, body=%wide.region_16.19_spmd.clone.sunk | while | flops 6491146752 | bytes 86845712 | solution.py:46
  937.3 37.8 %all-gather.14.cloned.1.call-done = bf16[16,32,1024]{2,1,0:T(8,128)(2,1)} async-done(((bf16[1,32,1024]{2,1,0:T(8,128)(2,1)}), bf16[16,32,1024]{2,1,0:T(8,128)(2,1)}) %all-gather.14.cloned.1.call-update) | async-done | bytes 1048592 | tf_op jit(solution)/shard_map/while/body/eval_jaxpr/all_gather | solution.py:36
  996.6 41.3 %reduce-scatter.5.cloned.1.call-done = bf16[1,32,1024]{2,1,0:T(8,128)(2,1)} async-done(((bf16[16,32,1024]{2,1,0:T(8,128)(2,1)}), bf16[1,32,1024]{2,1,0:T(8,128)(2,1)}) %reduce-scatter.5.cloned.1.call-update) | async-done | bytes 65552 | tf_op jit(solution)/shard_map/while/body/eval_jaxpr/reduce_scatter | solution.py:44
  1042.0 37.5 %all-gather.14.cloned.1.call-done = bf16[16,32,1024]{2,1,0:T(8,128)(2,1)} async-done(((bf16[1,32,1024]{2,1,0:T(8,128)(2,1)}), bf16[16,32,1024]{2,1,0:T(8,128)(2,1)}) %all-gather.14.cloned.1.call-update) | async-done | bytes 1048592 | tf_op jit(solution)/shard_map/while/body/eval_jaxpr/all_gather | solution.py:36
  1103.4 38.9 %reduce-scatter.5.cloned.1.call-done = bf16[1,32,1024]{2,1,0:T(8,128)(2,1)} async-done(((bf16[16,32,1024]{2,1,0:T(8,128)(2,1)}), bf16[1,32,1024]{2,1,0:T(8,128)(2,1)}) %reduce-scatter.5.cloned.1.call-update) | async-done | bytes 65552 | tf_op jit(solution)/shard_map/while/body/eval_jaxpr/reduce_scatter | solution.py:44
  1146.3 37.7 %all-gather.14.cloned.1.call-done = bf16[16,32,1024]{2,1,0:T(8,128)(2,1)} async-done(((bf16[1,32,1024]{2,1,0:T(8,128)(2,1)}), bf16[16,32,1024]{2,1,0:T(8,128)(2,1)}) %all-gather.14.cloned.1.call-update) | async-done | bytes 1048592 | tf_op jit(solution)/shard_map/while/body/eval_jaxpr/all_gather | solution.py:36
  1207.9 38.9 %reduce-scatter.5.cloned.1.call-done = bf16[1,32,1024]{2,1,0:T(8,128)(2,1)} async-done(((bf16[16,32,1024]{2,1,0:T(8,128)(2,1)}), bf16[1,32,1024]{2,1,0:T(8,128)(2,1)}) %reduce-scatter.5.cloned.1.call-update) | async-done | bytes 65552 | tf_op jit(solution)/shard_map/while/body/eval_jaxpr/reduce_scatter | solution.py:44
  1250.8 37.8 %all-gather.14.cloned.1.call-done = bf16[16,32,1024]{2,1,0:T(8,128)(2,1)} async-done(((bf16[1,32,1024]{2,1,0:T(8,128)(2,1)}), bf16[16,32,1024]{2,1,0:T(8,128)(2,1)}) %all-gather.14.cloned.1.call-update) | async-done | bytes 1048592 | tf_op jit(solution)/shard_map/while/body/eval_jaxpr/all_gather | solution.py:36
  1312.4 38.9 %reduce-scatter.5.cloned.1.call-done = bf16[1,32,1024]{2,1,0:T(8,128)(2,1)} async-done(((bf16[16,32,1024]{2,1,0:T(8,128)(2,1)}), bf16[1,32,1024]{2,1,0:T(8,128)(2,1)}) %reduce-scatter.5.cloned.1.call-update) | async-done | bytes 65552 | tf_op jit(solution)/shard_map/while/body/eval_jaxpr/reduce_scatter | solution.py:44
  1416.4 39.1 %reduce-scatter.5.cloned.1.call-done = bf16[1,32,1024]{2,1,0:T(8,128)(2,1)} async-done(((bf16[16,32,1024]{2,1,0:T(8,128)(2,1)}), bf16[1,32,1024]{2,1,0:T(8,128)(2,1)}) %reduce-scatter.5.cloned.1.call-update) | async-done | bytes 65552 | tf_op jit(solution)/shard_map/while/body/eval_jaxpr/reduce_scatter | solution.py:44
  1520.8 38.9 %reduce-scatter.5.cloned.1.call-done = bf16[1,32,1024]{2,1,0:T(8,128)(2,1)} async-done(((bf16[16,32,1024]{2,1,0:T(8,128)(2,1)}), bf16[1,32,1024]{2,1,0:T(8,128)(2,1)}) %reduce-scatter.5.cloned.1.call-update) | async-done | bytes 65552 | tf_op jit(solution)/shard_map/while/body/eval_jaxpr/reduce_scatter | solution.py:44
  1563.7 37.6 %all-gather.14.cloned.1.call-done = bf16[16,32,1024]{2,1,0:T(8,128)(2,1)} async-done(((bf16[1,32,1024]{2,1,0:T(8,128)(2,1)}), bf16[16,32,1024]{2,1,0:T(8,128)(2,1)}) %all-gather.14.cloned.1.call-update) | async-done | bytes 1048592 | tf_op jit(solution)/shard_map/while/body/eval_jaxpr/all_gather | solution.py:36
  1625.1 38.9 %reduce-scatter.5.cloned.1.call-done = bf16[1,32,1024]{2,1,0:T(8,128)(2,1)} async-done(((bf16[16,32,1024]{2,1,0:T(8,128)(2,1)}), bf16[1,32,1024]{2,1,0:T(8,128)(2,1)}) %reduce-scatter.5.cloned.1.call-update) | async-done | bytes 65552 | tf_op jit(solution)/shard_map/while/body/eval_jaxpr/reduce_scatter | solution.py:44
  1729.1 39.1 %reduce-scatter.5.cloned.1.call-done = bf16[1,32,1024]{2,1,0:T(8,128)(2,1)} async-done(((bf16[16,32,1024]{2,1,0:T(8,128)(2,1)}), bf16[1,32,1024]{2,1,0:T(8,128)(2,1)}) %reduce-scatter.5.cloned.1.call-update) | async-done | bytes 65552 | tf_op jit(solution)/shard_map/while/body/eval_jaxpr/reduce_scatter | solution.py:44
  1772.2 37.4 %all-gather.14.cloned.1.call-done = bf16[16,32,1024]{2,1,0:T(8,128)(2,1)} async-done(((bf16[1,32,1024]{2,1,0:T(8,128)(2,1)}), bf16[16,32,1024]{2,1,0:T(8,128)(2,1)}) %all-gather.14.cloned.1.call-update) | async-done | bytes 1048592 | tf_op jit(solution)/shard_map/while/body/eval_jaxpr/all_gather | solution.py:36
  1833.5 39.1 %reduce-scatter.5.cloned.1.call-done = bf16[1,32,1024]{2,1,0:T(8,128)(2,1)} async-done(((bf16[16,32,1024]{2,1,0:T(8,128)(2,1)}), bf16[1,32,1024]{2,1,0:T(8,128)(2,1)}) %reduce-scatter.5.cloned.1.call-update) | async-done | bytes 65552 | tf_op jit(solution)/shard_map/while/body/eval_jaxpr/reduce_scatter | solution.py:44
  1937.5 38.9 %reduce-scatter.5.cloned.1.call-done = bf16[1,32,1024]{2,1,0:T(8,128)(2,1)} async-done(((bf16[16,32,1024]{2,1,0:T(8,128)(2,1)}), bf16[1,32,1024]{2,1,0:T(8,128)(2,1)}) %reduce-scatter.5.cloned.1.call-update) | async-done | bytes 65552 | tf_op jit(solution)/shard_map/while/body/eval_jaxpr/reduce_scatter | solution.py:44
  2041.5 38.9 %reduce-scatter.5.cloned.1.call-done = bf16[1,32,1024]{2,1,0:T(8,128)(2,1)} async-done(((bf16[16,32,1024]{2,1,0:T(8,128)(2,1)}), bf16[1,32,1024]{2,1,0:T(8,128)(2,1)}) %reduce-scatter.5.cloned.1.call-update) | async-done | bytes 65552 | tf_op jit(solution)/shard_map/while/body/eval_jaxpr/reduce_scatter | solution.py:44
  2084.5 37.5 %all-gather.14.cloned.1.call-done = bf16[16,32,1024]{2,1,0:T(8,128)(2,1)} async-done(((bf16[1,32,1024]{2,1,0:T(8,128)(2,1)}), bf16[16,32,1024]{2,1,0:T(8,128)(2,1)}) %all-gather.14.cloned.1.call-update) | async-done | bytes 1048592 | tf_op jit(solution)/shard_map/while/body/eval_jaxpr/all_gather | solution.py:36
  2145.9 39.0 %reduce-scatter.5.cloned.1.call-done = bf16[1,32,1024]{2,1,0:T(8,128)(2,1)} async-done(((bf16[16,32,1024]{2,1,0:T(8,128)(2,1)}), bf16[1,32,1024]{2,1,0:T(8,128)(2,1)}) %reduce-scatter.5.cloned.1.call-update) | async-done | bytes 65552 | tf_op jit(solution)/shard_map/while/body/eval_jaxpr/reduce_scatter | solution.py:44
  2249.9 39.1 %reduce-scatter.5.cloned.1.call-done = bf16[1,32,1024]{2,1,0:T(8,128)(2,1)} async-done(((bf16[16,32,1024]{2,1,0:T(8,128)(2,1)}), bf16[1,32,1024]{2,1,0:T(8,128)(2,1)}) %reduce-scatter.5.cloned.1.call-update) | async-done | bytes 65552 | tf_op jit(solution)/shard_map/while/body/eval_jaxpr/reduce_scatter | solution.py:44
  2353.9 38.9 %reduce-scatter.5.cloned.1.call-done = bf16[1,32,1024]{2,1,0:T(8,128)(2,1)} async-done(((bf16[16,32,1024]{2,1,0:T(8,128)(2,1)}), bf16[1,32,1024]{2,1,0:T(8,128)(2,1)}) %reduce-scatter.5.cloned.1.call-update) | async-done | bytes 65552 | tf_op jit(solution)/shard_map/while/body/eval_jaxpr/reduce_scatter | solution.py:44
  2457.9 38.9 %reduce-scatter.5.cloned.1.call-done = bf16[1,32,1024]{2,1,0:T(8,128)(2,1)} async-done(((bf16[16,32,1024]{2,1,0:T(8,128)(2,1)}), bf16[1,32,1024]{2,1,0:T(8,128)(2,1)}) %reduce-scatter.5.cloned.1.call-update) | async-done | bytes 65552 | tf_op jit(solution)/shard_map/while/body/eval_jaxpr/reduce_scatter | solution.py:44
  2562.0 38.9 %reduce-scatter.5.cloned.1.call-done = bf16[1,32,1024]{2,1,0:T(8,128)(2,1)} async-done(((bf16[16,32,1024]{2,1,0:T(8,128)(2,1)}), bf16[1,32,1024]{2,1,0:T(8,128)(2,1)}) %reduce-scatter.5.cloned.1.call-update) | async-done | bytes 65552 | tf_op jit(solution)/shard_map/while/body/eval_jaxpr/reduce_scatter | solution.py:44
  2604.0 264.3 %while.51 = (s32[]{:T(128)}, f32[1024,2048]{1,0:T(8,128)}, f32[2048]{0:T(1024)S(1)}, bf16[2,128,1024]{2,1,0:T(8,128)(2,1)}, bf16[2,128,1024]{2,1,0:T(8,128)(2,1)...) while((s32[]{:T(128)}, f32[1024,2048]{1,0:T(8,128)}, ...), condition=%wide.region_23.24_spmd, body=%wide.region_20.23_spmd.sunk | while | flops 25949898752 | bytes 173252928 | solution.py:46
  2605.2 42.2 %all-gather.12.cloned.1.call-done = bf16[16,128,1024]{2,1,0:T(8,128)(2,1)} async-done(((bf16[1,128,1024]{2,1,0:T(8,128)(2,1)}), bf16[16,128,1024]{2,1,0:T(8,128)(2,1)}) %all-gather.12.cloned.1.call-update) | async-done | bytes 4194320 | tf_op jit(solution)/shard_map/while/body/eval_jaxpr/all_gather | solution.py:36
  2737.0 42.7 %all-gather.12.cloned.1.call-done = bf16[16,128,1024]{2,1,0:T(8,128)(2,1)} async-done(((bf16[1,128,1024]{2,1,0:T(8,128)(2,1)}), bf16[16,128,1024]{2,1,0:T(8,128)(2,1)}) %all-gather.12.cloned.1.call-update) | async-done | bytes 4194320 | tf_op jit(solution)/shard_map/while/body/eval_jaxpr/all_gather | solution.py:36
  (519 shorter events, 1765.2 us)
Async XLA Ops:
  746.3 41.0 %all-gather.10.cloned.1.call-start = ((), (), s32[]{:S(2)}) async-start(), calls=%async_computation.3 | async-start | bytes 4456448 | tf_op jit(solution)/shard_map/while/body/eval_jaxpr/all_gather | solution.py:23
  934.6 40.6 %all-gather.14.cloned.1.call-start = ((), (), s32[]{:S(2)}) async-start(), calls=%async_computation.6 | async-start | bytes 1114112 | tf_op jit(solution)/shard_map/while/body/eval_jaxpr/all_gather | solution.py:36
  936.3 101.6 %reduce-scatter.5.cloned.1.call-start = ((), (), s32[]{:S(2)}) async-start(), calls=%async_computation.7 | async-start | bytes 1114112 | tf_op jit(solution)/shard_map/while/body/eval_jaxpr/reduce_scatter | solution.py:44
  1039.4 40.1 %all-gather.14.cloned.1.call-start = ((), (), s32[]{:S(2)}) async-start(), calls=%async_computation.6 | async-start | bytes 1114112 | tf_op jit(solution)/shard_map/while/body/eval_jaxpr/all_gather | solution.py:36
  1040.9 101.3 %reduce-scatter.5.cloned.1.call-start = ((), (), s32[]{:S(2)}) async-start(), calls=%async_computation.7 | async-start | bytes 1114112 | tf_op jit(solution)/shard_map/while/body/eval_jaxpr/reduce_scatter | solution.py:44
  1143.7 40.3 %all-gather.14.cloned.1.call-start = ((), (), s32[]{:S(2)}) async-start(), calls=%async_computation.6 | async-start | bytes 1114112 | tf_op jit(solution)/shard_map/while/body/eval_jaxpr/all_gather | solution.py:36
  1145.3 101.5 %reduce-scatter.5.cloned.1.call-start = ((), (), s32[]{:S(2)}) async-start(), calls=%async_computation.7 | async-start | bytes 1114112 | tf_op jit(solution)/shard_map/while/body/eval_jaxpr/reduce_scatter | solution.py:44
  1248.2 40.3 %all-gather.14.cloned.1.call-start = ((), (), s32[]{:S(2)}) async-start(), calls=%async_computation.6 | async-start | bytes 1114112 | tf_op jit(solution)/shard_map/while/body/eval_jaxpr/all_gather | solution.py:36
  1249.8 101.5 %reduce-scatter.5.cloned.1.call-start = ((), (), s32[]{:S(2)}) async-start(), calls=%async_computation.7 | async-start | bytes 1114112 | tf_op jit(solution)/shard_map/while/body/eval_jaxpr/reduce_scatter | solution.py:44
  1352.8 39.8 %all-gather.14.cloned.1.call-start = ((), (), s32[]{:S(2)}) async-start(), calls=%async_computation.6 | async-start | bytes 1114112 | tf_op jit(solution)/shard_map/while/body/eval_jaxpr/all_gather | solution.py:36
  1354.3 101.2 %reduce-scatter.5.cloned.1.call-start = ((), (), s32[]{:S(2)}) async-start(), calls=%async_computation.7 | async-start | bytes 1114112 | tf_op jit(solution)/shard_map/while/body/eval_jaxpr/reduce_scatter | solution.py:44
  1457.0 39.9 %all-gather.14.cloned.1.call-start = ((), (), s32[]{:S(2)}) async-start(), calls=%async_computation.6 | async-start | bytes 1114112 | tf_op jit(solution)/shard_map/while/body/eval_jaxpr/all_gather | solution.py:36
  1458.5 101.1 %reduce-scatter.5.cloned.1.call-start = ((), (), s32[]{:S(2)}) async-start(), calls=%async_computation.7 | async-start | bytes 1114112 | tf_op jit(solution)/shard_map/while/body/eval_jaxpr/reduce_scatter | solution.py:44
  1561.1 40.1 %all-gather.14.cloned.1.call-start = ((), (), s32[]{:S(2)}) async-start(), calls=%async_computation.6 | async-start | bytes 1114112 | tf_op jit(solution)/shard_map/while/body/eval_jaxpr/all_gather | solution.py:36
  1562.7 101.3 %reduce-scatter.5.cloned.1.call-start = ((), (), s32[]{:S(2)}) async-start(), calls=%async_computation.7 | async-start | bytes 1114112 | tf_op jit(solution)/shard_map/while/body/eval_jaxpr/reduce_scatter | solution.py:44
  1665.5 39.8 %all-gather.14.cloned.1.call-start = ((), (), s32[]{:S(2)}) async-start(), calls=%async_computation.6 | async-start | bytes 1114112 | tf_op jit(solution)/shard_map/while/body/eval_jaxpr/all_gather | solution.py:36
  1667.0 101.2 %reduce-scatter.5.cloned.1.call-start = ((), (), s32[]{:S(2)}) async-start(), calls=%async_computation.7 | async-start | bytes 1114112 | tf_op jit(solution)/shard_map/while/body/eval_jaxpr/reduce_scatter | solution.py:44
  1769.7 39.9 %all-gather.14.cloned.1.call-start = ((), (), s32[]{:S(2)}) async-start(), calls=%async_computation.6 | async-start | bytes 1114112 | tf_op jit(solution)/shard_map/while/body/eval_jaxpr/all_gather | solution.py:36
  1771.2 101.3 %reduce-scatter.5.cloned.1.call-start = ((), (), s32[]{:S(2)}) async-start(), calls=%async_computation.7 | async-start | bytes 1114112 | tf_op jit(solution)/shard_map/while/body/eval_jaxpr/reduce_scatter | solution.py:44
  1875.6 100.8 %reduce-scatter.5.cloned.1.call-start = ((), (), s32[]{:S(2)}) async-start(), calls=%async_computation.7 | async-start | bytes 1114112 | tf_op jit(solution)/shard_map/while/body/eval_jaxpr/reduce_scatter | solution.py:44
  1977.8 39.8 %all-gather.14.cloned.1.call-start = ((), (), s32[]{:S(2)}) async-start(), calls=%async_computation.6 | async-start | bytes 1114112 | tf_op jit(solution)/shard_map/while/body/eval_jaxpr/all_gather | solution.py:36
  1979.4 101.0 %reduce-scatter.5.cloned.1.call-start = ((), (), s32[]{:S(2)}) async-start(), calls=%async_computation.7 | async-start | bytes 1114112 | tf_op jit(solution)/shard_map/while/body/eval_jaxpr/reduce_scatter | solution.py:44
  2081.9 40.1 %all-gather.14.cloned.1.call-start = ((), (), s32[]{:S(2)}) async-start(), calls=%async_computation.6 | async-start | bytes 1114112 | tf_op jit(solution)/shard_map/while/body/eval_jaxpr/all_gather | solution.py:36
  2083.4 101.5 %reduce-scatter.5.cloned.1.call-start = ((), (), s32[]{:S(2)}) async-start(), calls=%async_computation.7 | async-start | bytes 1114112 | tf_op jit(solution)/shard_map/while/body/eval_jaxpr/reduce_scatter | solution.py:44
  2187.9 101.0 %reduce-scatter.5.cloned.1.call-start = ((), (), s32[]{:S(2)}) async-start(), calls=%async_computation.7 | async-start | bytes 1114112 | tf_op jit(solution)/shard_map/while/body/eval_jaxpr/reduce_scatter | solution.py:44
  2292.0 100.8 %reduce-scatter.5.cloned.1.call-start = ((), (), s32[]{:S(2)}) async-start(), calls=%async_computation.7 | async-start | bytes 1114112 | tf_op jit(solution)/shard_map/while/body/eval_jaxpr/reduce_scatter | solution.py:44
  2395.8 101.0 %reduce-scatter.5.cloned.1.call-start = ((), (), s32[]{:S(2)}) async-start(), calls=%async_computation.7 | async-start | bytes 1114112 | tf_op jit(solution)/shard_map/while/body/eval_jaxpr/reduce_scatter | solution.py:44
  2499.8 101.0 %reduce-scatter.5.cloned.1.call-start = ((), (), s32[]{:S(2)}) async-start(), calls=%async_computation.7 | async-start | bytes 1114112 | tf_op jit(solution)/shard_map/while/body/eval_jaxpr/reduce_scatter | solution.py:44
  2604.2 43.2 %all-gather.12.cloned.1.call-start = ((), (), s32[]{:S(2)}) async-start(), calls=%async_computation.4 | async-start | bytes 4456448 | tf_op jit(solution)/shard_map/while/body/eval_jaxpr/all_gather | solution.py:36
  2605.1 129.2 %reduce-scatter.3.cloned.1.call-start = ((), (), s32[]{:S(2)}) async-start(), calls=%async_computation.5 | async-start | bytes 4456448 | tf_op jit(solution)/shard_map/while/body/eval_jaxpr/reduce_scatter | solution.py:44
  2736.1 43.6 %all-gather.12.cloned.1.call-start = ((), (), s32[]{:S(2)}) async-start(), calls=%async_computation.4 | async-start | bytes 4456448 | tf_op jit(solution)/shard_map/while/body/eval_jaxpr/all_gather | solution.py:36
  2736.9 129.7 %reduce-scatter.3.cloned.1.call-start = ((), (), s32[]{:S(2)}) async-start(), calls=%async_computation.5 | async-start | bytes 4456448 | tf_op jit(solution)/shard_map/while/body/eval_jaxpr/reduce_scatter | solution.py:44
  (80 other events, 13128.5 us)
Sparse Core Ops, SparseCore 0:
  749.1 38.2 all-gather.9
  937.6 37.5 all-gather.13
  987.8 50.0 reduce-scatter.4
  1042.4 37.0 all-gather.13
  1092.1 50.0 reduce-scatter.4
  1146.7 37.2 all-gather.13
  1196.7 50.0 reduce-scatter.4
  1251.2 37.2 all-gather.13
  1301.2 50.0 reduce-scatter.4
  1355.5 37.0 all-gather.13
  1405.2 50.2 reduce-scatter.4
  1509.6 50.0 reduce-scatter.4
  1564.1 37.0 all-gather.13
  1613.9 50.0 reduce-scatter.4
  1668.2 37.0 all-gather.13
  1717.9 50.2 reduce-scatter.4
  1822.3 50.2 reduce-scatter.4
  1926.3 50.0 reduce-scatter.4
  1980.5 37.0 all-gather.13
  2030.3 50.0 reduce-scatter.4
  2084.9 37.0 all-gather.13
  2134.7 50.2 reduce-scatter.4
  2238.7 50.2 reduce-scatter.4
  2342.7 50.0 reduce-scatter.4
  2397.0 37.0 all-gather.13
  2446.7 50.0 reduce-scatter.4
  2501.0 37.0 all-gather.13
  2550.8 50.0 reduce-scatter.4
  2606.9 40.4 all-gather.11
  2679.6 54.6 reduce-scatter.2
  2738.8 40.8 all-gather.11
  2811.8 54.7 reduce-scatter.2
  (22 shorter events, 759.2 us)
where the time goes:
time: 2890 us; the launch traced here: 2880 us
  waiting for transfers between devices  2000 us (69%)
  matrix products  562 us (19%)
  local copies, waits for them, and re-layouts  147 us (5%)
  blocking collectives  94.5 us (3%)
  other arithmetic  53.1 us (2%)
    all_gather x36, waiting for transfers between devices, one_row(): gathered = lax.all_gather(hid_row, 'tp')  1320 us
    reduce_scatter x18, waiting for transfers between devices, one_row(): own_hid = lax.psum_scatter(part_hid, 'tp', scatter_dimension=0, tiled=True)  679 us
    dot_general x36, matrix products, head_logits(): jnp.einsum('pld,dv->plv', gathered, w_head, preferred_element_type=jnp.fl...  251 us
    dot_general x18, matrix products, one_row(): jnp.einsum('pld,plv->dv', gathered, grad_low, preferred_element_type=jnp....  217 us
    dot_general x18, matrix products, one_row(): jnp.einsum('plv,dv->pld', grad_low, w_head, preferred_element_type=jnp.fl...  89.3 us
  transfers between devices with their start and end apart: 54, of which 54 were waited for; matrix products, arithmetic and copies ran while one was open for 9% of the time, Pallas kernels for 0%

commit v1 on v0

v1 whole, which is shorter than its diff:
```python
import functools
import math
import jax
import jax.numpy as jnp
from jax import lax
from jax.experimental import pallas as pl
from jax.experimental.pallas import tpu as pltpu
from jax.sharding import PartitionSpec as P

MESH = pl.DeviceIdType.MESH
HIGHEST = lax.Precision.HIGHEST
F32 = jnp.float32
BF16 = jnp.bfloat16

UT = 16
CH = 512
MAXD = 4


def kernel(n_group, q_rows, q_len, d_rows, d_len,
           q_ref, d_ref, w_ref, b_ref, msg_ref,
           loss_ref, gw_out, gb_ref, dq_out, dd_out,
           wbuf, wt, gw, grecv, rep, maskx, own, acc_h, part, xbuf, rbuf, sbuf, gbuf, pbuf, xt,
           rdx, ddx, ddr, bias, gbacc, gbrecv, msgs, smsg, lossx, lossf,
           ag_send, ag_recv, ag_cred, rs_send, rs_recv, rs_cred,
           loc_sem, w_sem, bias_sem, msg_send, msg_recv, sm_send, sm_recv, pair_sem, gx_send, gx_recv,
           loss_send, loss_recv, out_sem):
    nz = n_group // 2
    hid = w_ref.shape[0]
    v_loc = w_ref.shape[1]
    v_chip = 2 * v_loc
    n_q = q_rows * q_len // UT
    n_d = d_rows * d_len // UT
    n_unit = n_q + n_d
    per_row = q_len // UT
    pieces = d_len // q_len
    pad_rows = MAXD // per_row
    rows = nz * UT
    n_chunk = v_chip // CH

    me = lax.axis_index('tp')
    z = me // 2
    c = lax.rem(me, 2)
    right = lax.rem(z + 1, nz)
    left = lax.rem(z + nz - 1, nz)
    sib = {'tp': 2 * z + 1 - c}

    def same(zz):
        return {'tp': 2 * zz + c}

    ahead = (same(right), same(left))
    behind = (same(left), same(right))

    def slot(way, dist):
        return dist if way == 0 else nz - dist

    def dist_of(s):
        return min(s, nz - s)

    def chip_of(s):
        return lax.rem(z - s + nz, nz)

    def rows_of(s):
        return pl.ds(pl.multiple_of(chip_of(s) * UT, UT), UT)

    def far(chip):
        s = lax.rem(z - chip + nz, nz)
        return s - (s // (MAXD + 1)) * (2 * s - nz)

    peers = [same(lax.rem(z + t, nz)) for t in range(1, nz)]

    load_q = pltpu.make_async_copy(q_ref, own.at[pl.ds(0, n_q)], loc_sem.at[0])
    load_d = pltpu.make_async_copy(d_ref, own.at[pl.ds(n_q, n_d)], loc_sem.at[1])
    my_cols = pl.ds(pl.multiple_of(c * v_loc, v_loc), v_loc)
    sib_cols = pl.ds(pl.multiple_of((1 - c) * v_loc, v_loc), v_loc)
    load_w = pltpu.make_async_copy(w_ref, wbuf.at[:, my_cols], loc_sem.at[2])
    load_b = pltpu.make_async_copy(b_ref, bias.at[:, my_cols], loc_sem.at[3])
    load_m = pltpu.make_async_copy(msg_ref, msgs.at[z], loc_sem.at[4])
    for cp in (load_q, load_d, load_w, load_b, load_m):
        cp.start()
    xbuf[...] = jnp.zeros_like(xbuf)

    barrier = pltpu.get_barrier_semaphore()
    for dev in [sib] + peers:
        pl.semaphore_signal(barrier, inc=1, device_id=dev, device_id_type=MESH)
    pl.semaphore_wait(barrier, nz)

    send_m = [pltpu.make_async_remote_copy(msg_ref, msgs.at[z], msg_send.at[t], msg_recv.at[t], device_id=peers[t - 1],
                                           device_id_type=MESH) for t in range(1, nz)]
    for cp in send_m:
        cp.start()
    send_w = pltpu.make_async_remote_copy(w_ref, wbuf.at[:, my_cols], w_sem.at[0], w_sem.at[1], device_id=sib,
                                          device_id_type=MESH)
    send_w.start()
    send_b = pltpu.make_async_remote_copy(b_ref, bias.at[:, my_cols], bias_sem.at[0], bias_sem.at[1], device_id=sib,
                                          device_id_type=MESH)
    send_b.start()
    load_q.wait()
    load_d.wait()
    load_m.wait()

    @pl.loop(0, rep.shape[0])
    def _(i):
        rep[i] = jnp.zeros(rep.shape[1:], F32)

    @pl.loop(0, maskx.shape[0])
    def _(i):
        maskx[i] = jnp.zeros(maskx.shape[1:], F32)
    gbacc[...] = jnp.zeros_like(gbacc)

    @pl.loop(0, hid // 64)
    def _(i):
        gw[pl.ds(pl.multiple_of(i * 64, 64), 64), :] = jnp.zeros((64, v_chip), F32)

    for cp in send_m:
        cp.wait()

    units_in_row = 128 // UT
    for s in range(nz):
        for r in range(n_unit // units_in_row):
            tile = jnp.broadcast_to(msgs[chip_of(s), r:r + 1, :], (128, 128)).T
            for i in range(units_in_row):
                maskx[r * units_in_row + i + dist_of(s), rows_of(s), :] = tile[i * UT:(i + 1) * UT, :]

    load_w.wait()
    load_b.wait()

    def in_range(n):
        return (n >= 0) & (n < n_unit)

    def carries(way, dist, n):
        ok = in_range(n)
        if dist == MAXD:
            ok = ok & (lax.rem(n + 2 * n_unit, 2) == way)
        return ok

    def rows_there(way, dist):
        return rows_of(slot(way, dist - 1) if dist > 1 else 0)

    def ag_copy(j, way, dist):
        n = j - (dist - 1)
        b = lax.rem(j, 2)
        here = xbuf.at[b, rows_of(slot(way, dist - 1))] if dist > 1 else own.at[n]
        s = slot(way, dist)
        return pltpu.make_async_remote_copy(here, xbuf.at[1 - b, rows_there(way, dist)], ag_send.at[way, dist - 1],
                                            ag_recv.at[1 - b, s], device_id=ahead[way], device_id_type=MESH)

    def ag_start(j, way, dist):
        n = j - (dist - 1)

        @pl.when(carries(way, dist, n) & (n >= 2 - dist))
        def _():
            pl.semaphore_wait(ag_cred.at[way, dist - 1], 1)

        @pl.when(carries(way, dist, n))
        def _():
            ag_copy(j, way, dist).start()

    def ag_arrive(j, way, dist):
        @pl.when(carries(way, dist, j - dist))
        def _():
            ag_copy(j - 1, way, dist).wait_recv()

    def ag_service(j):
        ag_start(j, 0, 1)
        ag_start(j, 1, 1)
        for dist in range(1, MAXD + 1):
            for way in (0, 1):
                ag_arrive(j, way, dist)
                if dist < MAXD:
                    ag_start(j, way, dist + 1)

        @pl.when(in_range(j))
        def _():
            xbuf[lax.rem(j, 2), rows_of(0)] = own[j]

    def ag_release(j):
        for dist in range(1, MAXD + 1):
            for way in (0, 1):
                @pl.when(carries(way, dist, j - (dist - 1)))
                def _():
                    ag_copy(j, way, dist).wait_send()
        for dist in range(1, MAXD + 1):
            for way in (0, 1):
                n = j - dist + 2

                @pl.when(carries(way, dist, n))
                def _():
                    pl.semaphore_signal(ag_cred.at[way, dist - 1], inc=1, device_id=behind[way], device_id_type=MESH)

    dists = [far(a) for a in range(nz)]

    def rep_row(j, a):
        return (j - dists[a] + MAXD) // per_row

    def fwd_chunk(j, b, c0):
        cols = pl.ds(c0, CH)
        logits = jnp.dot(xbuf[b], wbuf[:, cols], preferred_element_type=F32)
        for t in range(CH // 128):
            at = pl.ds(c0 + t * 128, 128)
            zt = logits[:, t * 128:(t + 1) * 128] + bias[:, at]
            act = jnp.log(1.0 + jnp.maximum(zt, 0.0)) * maskx[j]
            for s in range(nz):
                row_sum = jnp.sum(act[s * UT:(s + 1) * UT, :], axis=0, keepdims=True)
                idx = rep_row(j, s)
                rep[idx, s:s + 1, at] = rep[idx, s:s + 1, at] + row_sum

    send_w.wait()
    send_b.wait()

    @pl.loop(0, n_unit + MAXD)
    def _(j):
        ag_service(j)
        b = lax.rem(j, 2)
        for k in range(n_chunk):
            fwd_chunk(j, b, k * CH)
        ag_release(j)

        @pl.when(j < v_chip // 128)
        def _():
            at = pl.ds(pl.multiple_of(j * 128, 128), 128)
            wt[at, :] = wbuf[:, at].T

    q_total = q_rows * n_group
    d_total = d_rows * n_group
    v_total = v_loc * n_group
    tau = q_len * math.sqrt(v_total * d_len) / 16.0
    lam_q = 4.0 / (v_total * q_len * q_len)
    lam_d = 4.0 / (v_total * d_len * d_len)
    nd = d_rows * nz
    nq = q_rows * nz
    q0 = pad_rows
    d0 = pad_rows + q_rows

    @pl.loop(0, n_chunk)
    def _(k):
        at = pl.ds(pl.multiple_of(k * CH, CH), CH)
        for r in range(d_rows):
            rdx[c, r * nz:(r + 1) * nz, at] = sum(rep[d0 + r * pieces + i, :, at] for i in range(pieces))
        rdx[c, nd:nd + nz, at] = sum(rep[q0 + i, :, at] for i in range(q_rows))

    def to_sib(src, dst, i):
        return pltpu.make_async_remote_copy(src, dst, pair_sem.at[i, 0], pair_sem.at[i, 1], device_id=sib, device_id_type=MESH)

    send_rd = to_sib(rdx.at[c], rdx.at[c], 0)
    send_rd.start()
    send_rd.wait()

    def d_reps(at):
        return jnp.concatenate([rdx[0, 0:nd, at], rdx[1, 0:nd, at]], axis=0)

    def q_mean_of(at):
        return jnp.sum(rdx[0, nd:nd + nz, at] + rdx[1, nd:nd + nz, at], axis=0, keepdims=True) * (1.0 / q_total)

    def d_mean_of(at):
        return jnp.sum(d_reps(at), axis=0, keepdims=True) * (1.0 / d_total)

    def lanes(v):
        return sum(v[:, t * 128:(t + 1) * 128] for t in range(CH // 128))

    def score_chunk(k, carry):
        s_acc, rq, rd = carry
        at = pl.ds(pl.multiple_of(k * CH, CH), CH)
        q_rep = rep[q0:q0 + q_rows, :, at].reshape(nq, CH)
        s_acc = s_acc + lax.dot_general(d_reps(at), q_rep, (((1,), (1,)), ((), ())), precision=HIGHEST,
                                        preferred_element_type=F32)
        qm, dm = q_mean_of(at), d_mean_of(at)
        return s_acc, rq + lanes(qm * qm), rd + lanes(dm * dm)

    score, reg_q, reg_d = lax.fori_loop(0, n_chunk, score_chunk,
                                        (jnp.zeros((2 * nd, nq), F32), jnp.zeros((1, 128), F32), jnp.zeros((1, 128), F32)))
    smsg[0, 0:2 * nd, 0:nq] = score
    smsg[0, 2 * nd:2 * nd + 1, :] = reg_q
    smsg[0, 2 * nd + 1:2 * nd + 2, :] = reg_d
    send_s = [pltpu.make_async_remote_copy(smsg.at[0], smsg.at[t], sm_send.at[t], sm_recv.at[t], device_id=peers[t - 1],
                                           device_id_type=MESH) for t in range(1, nz)]
    for cp in send_s:
        cp.start()

    pos_rows = jnp.concatenate([msgs[s, 7:8, :] for s in range(nz)], axis=0)
    spread = (lax.broadcasted_iota(jnp.int32, (128, nq), 0)
              == lax.broadcasted_iota(jnp.int32, (128, nq), 1) // nz).astype(F32)
    pos_all = jnp.dot(pos_rows, spread, precision=HIGHEST, preferred_element_type=F32)
    pick = (lax.broadcasted_iota(jnp.int32, (nz, nq), 1) % nz == lax.broadcasted_iota(jnp.int32, (nz, nq), 0))
    pos_row = jnp.sum(jnp.where(pick, pos_all, 0.0), axis=0, keepdims=True)
    ridx = lax.broadcasted_iota(jnp.int32, (2 * nd, nq), 0)
    doc = (2 * (ridx % nz) + ridx // nd) * d_rows + (ridx // nz) % d_rows
    target = (doc.astype(F32) == pos_row).astype(F32)

    for cp in send_s:
        cp.wait()
    total = smsg[0]
    for t in range(1, nz):
        total = total + smsg[t]
    scores = total[0:2 * nd, 0:nq] * (1.0 / tau)
    top = jnp.max(scores, axis=0, keepdims=True)
    log_norm = top + jnp.log(jnp.sum(jnp.exp(scores - top), axis=0, keepdims=True))
    row_loss = log_norm - jnp.sum(scores * target, axis=0, keepdims=True)
    loss_part = jnp.sum(row_loss, axis=1, keepdims=True)
    gt = (jnp.exp(scores - log_norm) - target) * (1.0 / (q_total * tau))
    g = gt.T
    lossx[c] = jnp.broadcast_to(loss_part, (8, 128))
    send_l = to_sib(lossx.at[c], lossx.at[c], 1)
    send_l.start()

    @pl.loop(0, n_chunk)
    def _(k):
        at = pl.ds(pl.multiple_of(k * CH, CH), CH)
        q_rep = rep[q0:q0 + q_rows, :, at].reshape(nq, CH)
        dp = jnp.dot(gt, q_rep, precision=HIGHEST, preferred_element_type=F32)
        ddx[0, :, at] = dp[0:nd]
        ddx[1, :, at] = dp[nd:2 * nd]
        gq = jnp.dot(g, d_reps(at), precision=HIGHEST, preferred_element_type=F32) + q_mean_of(at) * (2.0 * lam_q / q_total)
        rep[q0:q0 + q_rows, :, at] = gq.reshape(q_rows, nz, CH)

    send_dd = to_sib(ddx.at[1 - c], ddr, 2)
    send_dd.start()
    send_l.wait()
    reg = (jnp.sum(total[2 * nd:2 * nd + 1, :], axis=1, keepdims=True) * lam_q
           + jnp.sum(total[2 * nd + 1:2 * nd + 2, :], axis=1, keepdims=True) * lam_d)
    lossf[0] = (lossx[0] + lossx[1]) * (1.0 / q_total) + reg

    send_loss = [pltpu.make_async_remote_copy(lossf.at[0], lossf.at[1], loss_send.at[t], loss_recv, device_id=peers[t - 1],
                                              device_id_type=MESH) for t in range(1, nz)]

    @pl.when(z == 0)
    def _():
        for cp in send_loss:
            cp.start()
    send_dd.wait()

    @pl.loop(0, n_chunk)
    def _(k):
        at = pl.ds(pl.multiple_of(k * CH, CH), CH)
        gd = ddx[c, :, at] + ddr[:, at] + d_mean_of(at) * (2.0 * lam_d / d_total)
        for r in range(d_rows):
            for i in range(pieces):
                rep[d0 + r * pieces + i, :, at] = gd[r * nz:(r + 1) * nz]

    def bwd_chunk(j, b, c0):
        cols = pl.ds(c0, CH)
        logits = jnp.dot(xbuf[b], wbuf[:, cols], preferred_element_type=F32)
        low = []
        for t in range(CH // 128):
            at = pl.ds(c0 + t * 128, 128)
            zt = logits[:, t * 128:(t + 1) * 128] + bias[:, at]
            grad = jnp.concatenate([jnp.broadcast_to(rep[rep_row(j, s), s:s + 1, at], (UT, 128)) for s in range(nz)], axis=0)
            gz = jnp.where(zt > 0.0, grad * maskx[j] / (1.0 + jnp.maximum(zt, 0.0)), 0.0)
            gbacc[:, at] = gbacc[:, at] + jnp.sum(gz.reshape(rows // 8, 8, 128), axis=0)
            low.append(gz.astype(BF16))
        low = jnp.concatenate(low, axis=1)
        gbuf[:, cols] = low
        gw[:, cols] = gw[:, cols] + jnp.dot(xt[...], low, preferred_element_type=F32)

    def bwd_hidden():
        for k in range(hid // 256 if hid >= 256 else 1):
            cols = pl.ds(k * 256, min(256, hid))
            pbuf[:, cols] = jnp.dot(gbuf[...], wt[:, cols], preferred_element_type=F32).astype(BF16)

    def rs_unit(j, dist):
        return j - (2 * MAXD - dist)

    def rs_copy(n, way, dist):
        return pltpu.make_async_remote_copy(sbuf.at[way, dist - 1], rbuf.at[way, dist - 1, lax.rem(n + 2 * n_unit, 2)],
                                            rs_send.at[way, dist - 1],
                                            rs_recv.at[way, dist - 1, lax.rem(n + 2 * n_unit, 2)],
                                            device_id=behind[way], device_id_type=MESH)

    def rs_take(n, way, dist):
        rs_copy(n, way, dist + 1).wait_recv()
        return rbuf[way, dist, lax.rem(n + 2 * n_unit, 2)].astype(F32)

    def rs_credit(n, way, dist):
        @pl.when(n + 2 < n_unit)
        def _():
            pl.semaphore_signal(rs_cred.at[way, dist], inc=1, device_id=ahead[way], device_id_type=MESH)

    def rs_send_on(n, way, dist):
        @pl.when(n >= 2)
        def _():
            pl.semaphore_wait(rs_cred.at[way, dist - 1], 1)
        rs_copy(n, way, dist).start()

    def rs_step(j):
        for dist in range(MAXD, 0, -1):
            for way in (0, 1):
                n_before = rs_unit(j - 1, dist)

                @pl.when(carries(way, dist, n_before))
                def _():
                    rs_copy(n_before, way, dist).wait_send()
        for dist in range(MAXD, 0, -1):
            for way in (0, 1):
                n = rs_unit(j, dist)
                s = slot(way, dist)
                if dist == MAXD:
                    @pl.when(carries(way, dist, n))
                    def _():
                        sbuf[way, dist - 1] = pbuf[rows_of(s), :]
                        rs_send_on(n, way, dist)
                elif dist == MAXD - 1:
                    @pl.when(in_range(n) & carries(way, dist + 1, n))
                    def _():
                        mine = part[s, lax.rem(n, 8)].astype(F32)
                        sbuf[way, dist - 1] = (mine + rs_take(n, way, dist)).astype(BF16)
                        rs_credit(n, way, dist)
                        rs_send_on(n, way, dist)

                    @pl.when(in_range(n) & jnp.logical_not(carries(way, dist + 1, n)))
                    def _():
                        sbuf[way, dist - 1] = part[s, lax.rem(n, 8)]
                        rs_send_on(n, way, dist)
                else:
                    @pl.when(in_range(n))
                    def _():
                        mine = part[s, lax.rem(n, 8)].astype(F32)
                        sbuf[way, dist - 1] = (mine + rs_take(n, way, dist)).astype(BF16)
                        rs_credit(n, way, dist)
                        rs_send_on(n, way, dist)
        home = rs_unit(j, 0)

        @pl.when(in_range(home))
        def _():
            acc_h[home] = (acc_h[home].astype(F32) + rs_take(home, 0, 0) + rs_take(home, 1, 0)).astype(BF16)
            rs_credit(home, 0, 0)
            rs_credit(home, 1, 0)

    @pl.loop(0, n_unit + 2 * MAXD)
    def _(j):
        @pl.when(j < n_unit + MAXD)
        def _():
            ag_service(j)
            b = lax.rem(j, 2)
            xt[...] = xbuf[b].T
            for k in range(n_chunk):
                bwd_chunk(j, b, k * CH)
            ag_release(j)
            bwd_hidden()
            for s in range(1, nz):
                if s != MAXD:
                    n = j - dist_of(s)
                    part[s, lax.rem(n + 8, 8)] = pbuf[rows_of(s), :]

            @pl.when(in_range(j))
            def _():
                acc_h[j] = pbuf[rows_of(0), :]
        rs_step(j)

    out_q = pltpu.make_async_copy(acc_h.at[pl.ds(0, n_q)], dq_out, out_sem.at[0])
    out_d = pltpu.make_async_copy(acc_h.at[pl.ds(n_q, n_d)], dd_out, out_sem.at[1])
    out_q.start()
    out_d.start()
    n_part = gx_send.shape[0] - 1
    step = v_loc // n_part
    send_g = []
    for k in range(n_part):
        theirs = pl.ds(pl.multiple_of((1 - c) * v_loc + k * step, step), step)
        send_g.append(pltpu.make_async_remote_copy(gw.at[:, theirs], grecv.at[:, pl.ds(k * step, step)], gx_send.at[k],
                                                   gx_recv.at[k], device_id=sib, device_id_type=MESH))
    send_gb = pltpu.make_async_remote_copy(gbacc.at[:, sib_cols], gbrecv, gx_send.at[n_part], gx_recv.at[n_part], device_id=sib,
                                           device_id_type=MESH)
    for cp in send_g:
        cp.start()
    send_gb.start()
    outs = []
    for k in range(n_part):
        send_g[k].wait_recv()
        at = pl.ds(pl.multiple_of(c * v_loc + k * step, step), step)

        @pl.loop(0, hid // 64)
        def _(i):
            rr = pl.ds(pl.multiple_of(i * 64, 64), 64)
            wbuf[rr, at] = (gw[rr, at] + grecv[rr, pl.ds(k * step, step)]).astype(BF16)
        outs.append(pltpu.make_async_copy(wbuf.at[:, at], gw_out.at[:, pl.ds(k * step, step)], out_sem.at[2 + k]))
        outs[-1].start()
    send_gb.wait_recv()
    gb_ref[...] = jnp.sum(gbacc[:, my_cols] + gbrecv[...], axis=0, keepdims=True)

    @pl.when(z == 0)
    def _():
        for cp in send_loss:
            cp.wait_send()
        loss_ref[...] = lossf[0]

    @pl.when(z != 0)
    def _():
        send_loss[0].wait_recv()
        loss_ref[...] = lossf[1]
    for cp in send_g:
        cp.wait_send()
    send_gb.wait_send()
    out_q.wait()
    out_d.wait()
    for cp in outs:
        cp.wait()


def solution(mesh):
    n_group = mesh.shape['tp']
    nz = n_group // 2
    row_spec = P(('dp', 'tp'))
    mask_spec = P(('dp', 'tp'), None)
    hid_spec = P(('dp', 'tp'), None, None)

    def local_step(q_hidden, d_hidden, q_mask, d_mask, positive, w_head, b_head):
        q_rows, q_len, hid = q_hidden.shape
        d_rows, d_len, _ = d_hidden.shape
        v_loc = w_head.shape[1]
        v_chip = 2 * v_loc
        n_q = q_rows * q_len // UT
        n_d = d_rows * d_len // UT
        n_unit = n_q + n_d
        per_row = q_len // UT
        rows = nz * UT
        nd, nq = d_rows * nz, q_rows * nz
        n_row = (n_unit + 2 * MAXD) // per_row
        flat = jnp.concatenate([q_mask.reshape(-1), d_mask.reshape(-1)]).astype(F32).reshape(-1, 128)
        pos = jnp.pad(positive.astype(F32), (0, 128 - q_rows)).reshape(1, 128)
        msg = jnp.concatenate([flat, jnp.zeros((7 - flat.shape[0], 128), F32), pos], axis=0)
        s_rows = -(-(2 * nd + 2) // 8) * 8
        n_part = 4
        dma, reg = pltpu.SemaphoreType.DMA, pltpu.SemaphoreType.REGULAR
        anym = pl.BlockSpec(memory_space=pl.ANY)
        vm = pl.BlockSpec(memory_space=pltpu.VMEM)
        out_shape = (
            jax.ShapeDtypeStruct((8, 128), F32),
            jax.ShapeDtypeStruct((hid, v_loc), BF16),
            jax.ShapeDtypeStruct((1, v_loc), F32),
            jax.ShapeDtypeStruct((n_q, UT, hid), BF16),
            jax.ShapeDtypeStruct((n_d, UT, hid), BF16),
        )
        scratch = [
            pltpu.VMEM((hid, v_chip), BF16),
            pltpu.VMEM((v_chip, hid), BF16),
            pltpu.VMEM((hid, v_chip), F32),
            pltpu.VMEM((hid, v_loc), F32),
            pltpu.VMEM((n_row, nz, v_chip), F32),
            pltpu.VMEM((n_unit + MAXD, rows, 128), F32),
            pltpu.VMEM((n_unit, UT, hid), BF16),
            pltpu.VMEM((n_unit, UT, hid), BF16),
            pltpu.VMEM((nz, 8, UT, hid), BF16),
            pltpu.VMEM((2, rows, hid), BF16),
            pltpu.VMEM((2, MAXD, 2, UT, hid), BF16),
            pltpu.VMEM((2, MAXD, UT, hid), BF16),
            pltpu.VMEM((rows, v_chip), BF16),
            pltpu.VMEM((rows, hid), BF16),
            pltpu.VMEM((hid, rows), BF16),
            pltpu.VMEM((2, nd + nz, v_chip), F32),
            pltpu.VMEM((2, nd, v_chip), F32),
            pltpu.VMEM((nd, v_chip), F32),
            pltpu.VMEM((1, v_chip), F32),
            pltpu.VMEM((8, v_chip), F32),
            pltpu.VMEM((8, v_loc), F32),
            pltpu.VMEM((nz, 8, 128), F32),
            pltpu.VMEM((nz, s_rows, 128), F32),
            pltpu.VMEM((2, 8, 128), F32),
            pltpu.VMEM((2, 8, 128), F32),
            dma((2, MAXD)), dma((2, nz)), reg((2, MAXD)),
            dma((2, MAXD)), dma((2, MAXD, 2)), reg((2, MAXD)),
            dma((5,)), dma((2,)), dma((2,)), dma((nz,)), dma((nz,)), dma((nz,)), dma((nz,)), dma((3, 2)),
            dma((n_part + 1,)), dma((n_part + 1,)), dma((nz,)), dma, dma((2 + n_part,)),
        ]
        loss, gw, gb, dq, dd = pl.pallas_call(
            functools.partial(kernel, n_group, q_rows, q_len, d_rows, d_len),
            out_shape=out_shape,
            in_specs=[anym] * 5,
            out_specs=(vm, anym, vm, anym, anym),
            scratch_shapes=scratch,
            compiler_params=pltpu.CompilerParams(collective_id=0, has_side_effects=True, vmem_limit_bytes=67043328),
        )(q_hidden.reshape(n_q, UT, hid), d_hidden.reshape(n_d, UT, hid), w_head, b_head.reshape(1, v_loc), msg)
        return (loss[0, 0:1], gw, gb.reshape(v_loc), dq.reshape(q_hidden.shape), dd.reshape(d_hidden.shape))

    return jax.shard_map(local_step, mesh=mesh,
                         in_specs=(hid_spec, hid_spec, mask_spec, mask_spec, row_spec, P(None, 'tp'), P('tp')),
                         out_specs=(P('dp'), P('dp', 'tp'), row_spec, hid_spec, hid_spec),
                         check_vma=False)
```

time: 2890 us -> 659 us (0.23)
  waiting for transfers between devices: 2000 us -> 0 us
  Pallas kernels: 0 us -> 647 us
  matrix products: 562 us -> 0 us
  local copies, waits for them, and re-layouts: 147 us -> 9.31 us
  blocking collectives: 94.5 us -> 0 us
  other arithmetic: 53.1 us -> 2.01 us
    all_gather x36 -> x0, waiting for transfers between devices: 1320 us -> none  [one_row(): gathered = lax.all_gather(hid_row, 'tp')]
    reduce_scatter x18 -> x0, waiting for transfers between devices: 679 us -> none  [one_row(): own_hid = lax.psum_scatter(part_hid, 'tp', scatter_dimension=0, tiled=True)]
    pallas_call x0 -> x1, Pallas kernels: none -> 647 us  [local_step(): pl.pallas_call(functools.partial(kernel, n_group, q_rows, q_len, d_rows,...]
    dot_general x75 -> x0, matrix products: 562 us -> none  [the longest x36 251 us: head_logits(): jnp.einsum('pld,dv->plv', gathered, w_head, preferred_element_type=jnp.fl...]
    dynamic_slice x36 -> x0, local copies, waits for them, and re-layouts: 50.2 us -> none  [side_reps(): row_reps = lax.map(one_row, (hidden, jnp.swapaxes(mask_all, 0, 1)))]
    psum x1 -> x0, blocking collectives: 44.3 us -> none  [local_step(): score_sum, reg_sum = lax.psum((score_part, reg_part), 'tp')]
    reduce_sum x22 -> x0, other arithmetic: 43.4 us -> none  [the longest x18 41 us: one_row(): acc_b = acc_b + jnp.sum(grad_logits, axis=(0, 1))]
    while x83 -> x0, local copies, waits for them, and re-layouts: 40.8 us -> none
  transfers between devices with their start and end apart: 54 -> 0, of which waited for: 54 -> 0; matrix products, arithmetic and copies ran while one was open for 9% -> 0% of each run, Pallas kernels for 0% -> 0%
where the time goes in v1:
time: 659 us
  Pallas kernels  647 us (98%)
  local copies, waits for them, and re-layouts  9.31 us (1%)
    pallas_call x1, Pallas kernels, local_step(): pl.pallas_call(functools.partial(kernel, n_group, q_rows, q_len, d_rows,...  647 us

profile of v1, /device:TPU:21, one launch (start us, length us, event | category | flops | bytes accessed | tf_op | source)
XLA Modules:
  0.0 659.1 jit_solution(7791807101406231297)
XLA Ops:
  0.6 0.7 convert_element_type.14
  1.3 0.1 pad.6.clone
  1.4 0.8 reshape.43
  2.1 0.7 fusion
  2.8 0.7 pad_maximum_fusion.msg_ref
  3.5 647.2 %shard_map.110 = (f32[8,128]{1,0:T(8,128)}, bf16[1024,2048]{1,0:T(8,128)(2,1)}, f32[1,2048]{1,0:T(1,128)}, bf16[32,16,1024]{2,1,0:T(8,128)(2,1)}, bf16[16,16,1024]{2,1,0:T(8,128)(2,1)}) custom-call(bf16[32,16,1024]{2,1,0:T(8,128)(2,1)} %bitcast.13, bf16[16,16,1024]{2,1,0:T(8,128)(2,1)} %bitcast.15, bf16[1024,2048]{1,0:T(8,128)(2,1)} %w_ref.1, ...), custom_call_target="tpu_custom_call" | custom-call | tf_op jit(solution)/shard_map/pallas_call | solution.py:563
  650.7 1.2 slice.3
  651.9 0.0 copy-start.2
  651.9 0.0 copy-start
  651.9 0.0 copy-start.1
  651.9 4.9 copy.16
  656.8 0.0 copy-done.2
  656.8 0.6 copy.17
  657.4 0.0 copy-done
  657.4 1.0 copy.18
  658.3 0.0 copy-done.1
  658.3 0.8 copy.19
  (1 shorter events, 0.0 us)
Async XLA Ops:
  651.9 4.9 copy-start.2
  651.9 5.5 copy-start
  651.9 6.5 copy-start.1

commit v2 on v0

v2 whole, which is shorter than its diff:
```python
import functools
import math
import jax
import jax.numpy as jnp
from jax import lax
from jax.experimental import pallas as pl
from jax.experimental.pallas import tpu as pltpu
from jax.sharding import PartitionSpec as P

MESH = pl.DeviceIdType.MESH
HIGHEST = lax.Precision.HIGHEST
F32 = jnp.float32
BF16 = jnp.bfloat16
BWD = UNROLL = True

UT = 16
CH = 512
MAXD = 4
KF = (1, 1, 2, 2, 3, 2, 1, 1)
KB = (1, 1, 1, 2, 2, 2, 1, 1)
LANE, SUB, PAIR, BIG = 128, 8, 2, 64
DEEP = 4
WAYS = (0, 1)
ORDER = (0, 1, 7, 2, 6, 3, 5, 4)
PAD = 4


def kernel(n_group, q_rows, q_len, d_rows, d_len,
           q_ref, d_ref, w_ref, b_ref, msg_ref,
           loss_ref, gw_out, gb_ref, dq_out, dd_out,
           wbuf, wt, gw, grecv, rep, maskx, own, acc_h, part, xbuf, rbuf, sbuf, hbuf, sibp, sst, gbuf, pbuf, xt,
           rdx, ddx, ddr, bias, gbacc, gbrecv, msgs, smsg, lossx, lossf,
           ag_send, ag_recv, ag_cred, inj_send, inj_cred, sib_send, sib_cred,
           rs_send, rs_recv, rs_cred, h_send, h_recv, h_cred, sp_send, sp_recv, sp_cred,
           loc_sem, w_sem, bias_sem, msg_send, msg_recv, sm_send, sm_recv, pair_sem, gx_send, gx_recv,
           loss_send, loss_recv, out_sem):
    ZERO = jnp.int32(0)
    nz = n_group // PAIR
    hid = w_ref.shape[0]
    v_loc = w_ref.shape[1]
    v_chip = PAIR * v_loc
    per_row = q_len // UT
    pieces = d_len // q_len
    n_qpage = q_rows // PAIR
    n_dpage = d_rows // PAIR * pieces
    n_page = n_qpage + n_dpage
    n_unit = n_page * per_row
    br = PAIR * UT
    rows = nz * br
    half = rows // PAIR
    n_chunk = v_chip // CH
    pos = {s: i for i, s in enumerate(ORDER)}

    me = lax.axis_index('tp')
    z = me // PAIR
    c = lax.rem(me, 2)
    o = 1 - c
    right = lax.rem(z + 1, nz)
    left = lax.rem(z + nz - 1, nz)

    def dev(zz, cc):
        return {'tp': PAIR * zz + cc}

    sib = dev(z, o)
    ahead = (right, left)
    behind = (left, right)

    def slot(way, dist):
        return dist if way == 0 else nz - dist

    def dist_of(s):
        return min(s, nz - s)

    def chip_of(s):
        return lax.rem(z - s + nz, nz)

    def block(s):
        return pl.ds(pos[s] * br, br)

    def part_of_block(s, i):
        return pl.ds(pl.multiple_of(pos[s] * br + i * UT, UT), UT)

    def par(n):
        return lax.rem(n + BIG, 2)

    def unit_rows(n):
        return pl.ds(pl.multiple_of(lax.rem(n, per_row) * UT, UT), UT)

    peers = [dev(lax.rem(z + t, nz), c) for t in range(1, nz)]
    others = [dev(lax.rem(z + t, nz), lax.rem(c + u, 2)) for t in range(nz) for u in WAYS if t or u]

    loads = []
    for cc in WAYS:
        loads.append(pltpu.make_async_copy(q_ref.at[:, cc], own.at[cc, pl.ds(0, n_qpage)], loc_sem.at[len(loads)]))
        for r in range(d_rows // PAIR):
            loads.append(pltpu.make_async_copy(d_ref.at[r, cc], own.at[cc, pl.ds(n_qpage + r * pieces, pieces)],
                                               loc_sem.at[len(loads)]))
    my_cols = pl.ds(pl.multiple_of(c * v_loc, v_loc), v_loc)
    sib_cols = pl.ds(pl.multiple_of(o * v_loc, v_loc), v_loc)
    load_m = pltpu.make_async_copy(msg_ref, msgs.at[me], loc_sem.at[len(loads)])
    load_w = pltpu.make_async_copy(w_ref, wbuf.at[:, my_cols], loc_sem.at[len(loads) + 1])
    load_b = pltpu.make_async_copy(b_ref, bias.at[:, my_cols], loc_sem.at[len(loads) + 2])
    for cp in loads + [load_m, load_w, load_b]:
        cp.start()
    xbuf[...] = jnp.zeros_like(xbuf)

    barrier = pltpu.get_barrier_semaphore()
    for d in others:
        pl.semaphore_signal(barrier, device_id=d, device_id_type=MESH)
    pl.semaphore_wait(barrier, n_group - 1)

    def remote(src, dst, ss, rs, to):
        return pltpu.make_async_remote_copy(src, dst, ss, rs, device_id=to, device_id_type=MESH)

    send_m = [remote(msg_ref, msgs.at[me], msg_send.at[k], msg_recv.at[k], d) for k, d in enumerate(others)]
    for cp in send_m:
        cp.start()
    for cp in loads:
        cp.wait()

    def carries(way, dist, n, stop=n_unit):
        ok = (n >= 0) & (n < stop)
        if dist == MAXD:
            ok = ok & (par(n) == way)
        return ok

    def credits_before(k, way, dist, n, bwd):
        later = n >= 3 - k[slot(way, dist) % nz]
        if not bwd:
            return [(later, 1)]
        if dist < MAXD:
            return [(n == 0, 2), (later, 1)]
        return [(n < 2, 1), (later, 1)]

    def wait_credit(sem, k, way, dist, n, bwd):
        for cond, amount in credits_before(k, way, dist, n, bwd):
            @pl.when(cond)
            def _():
                pl.semaphore_wait(sem, amount)

    def hop_copy(k, n, way, dist):
        s, s0 = slot(way, dist), slot(way, dist - 1)
        return remote(xbuf.at[par(n + k[s0]), block(s0)], xbuf.at[par(n + k[s]), block(s)],
                      ag_send.at[way, dist - 1, par(n)], ag_recv.at[par(n + k[s]), s, 0], dev(ahead[way], c))

    def inj_copy(k, n, way, cc, i):
        s = slot(way, 1)
        return remote(own.at[cc, n // per_row, unit_rows(n)], xbuf.at[par(n + k[s]), part_of_block(s, i)],
                      inj_send.at[way, cc], ag_recv.at[par(n + k[s]), s, i], dev(ahead[way], cc))

    def sib_copy(k, n):
        return remote(own.at[o, n // per_row, unit_rows(n)], xbuf.at[par(n + k[0]), part_of_block(0, c)],
                      sib_send, ag_recv.at[par(n + k[0]), 0, 0], sib)

    def inject(k, n, bwd=False):
        @pl.when((n >= 0) & (n < n_unit))
        def _():
            for cc in WAYS:
                for way in WAYS:
                    wait_credit(inj_cred.at[way, cc], k, way, 1, n, bwd)
                    inj_copy(k, n, way, cc, c).start()
            wait_credit(sib_cred, k, 0, 0, n, bwd)
            sib_copy(k, n).start()

    def injected(k, n):
        @pl.when((n >= 0) & (n < n_unit))
        def _():
            for cc in WAYS:
                for way in WAYS:
                    inj_copy(k, n, way, cc, c).wait_send()
            sib_copy(k, n).wait_send()

    def arrive(k, n, way, dist):
        @pl.when(carries(way, dist, n))
        def _():
            if dist == 0:
                sib_copy(k, n).wait_recv()
            elif dist == 1:
                for i in WAYS:
                    inj_copy(k, n, way, 0, i).wait_recv()
            else:
                hop_copy(k, n, way, dist).wait_recv()

    def forward(k, n, way, dist, bwd=False):
        @pl.when(carries(way, dist + 1, n))
        def _():
            wait_credit(ag_cred.at[way, dist], k, way, dist + 1, n, bwd)
            hop_copy(k, n, way, dist + 1).start()

    def relay(k, n, dist, bwd=False):
        for way in WAYS:
            arrive(k, n, way, dist)
            if dist < MAXD:
                forward(k, n, way, dist, bwd)

    def take_own(k, n):
        @pl.when((n >= 0) & (n < n_unit))
        def _():
            xbuf[par(n + k[0]), part_of_block(0, c)] = own[c, n // per_row, unit_rows(n)]

    def give_credit(way, dist, amount=1):
        if dist == 0:
            pl.semaphore_signal(sib_cred, inc=amount, device_id=sib, device_id_type=MESH)
        elif dist == 1:
            for i in WAYS:
                pl.semaphore_signal(inj_cred.at[way, c], inc=amount, device_id=dev(behind[way], i), device_id_type=MESH)
        else:
            pl.semaphore_signal(ag_cred.at[way, dist - 1], inc=amount, device_id=dev(behind[way], c), device_id_type=MESH)

    def lanes_of(s):
        if s == 0:
            return ((0, 0),)
        if s == MAXD:
            return ((0, MAXD), (1, MAXD))
        return ((0, s),) if s < MAXD else ((1, nz - s),)

    def release(k, j, slots):
        for s in slots:
            for way, dist in lanes_of(s):
                n = j - k[s]
                if 1 <= dist < MAXD:
                    @pl.when(carries(way, dist + 1, n))
                    def _():
                        hop_copy(k, n, way, dist + 1).wait_send()
        for s in slots:
            for way, dist in lanes_of(s):
                @pl.when(carries(way, dist, j - k[s] + 2))
                def _():
                    give_credit(way, dist)

    near, far = ORDER[:nz // PAIR], ORDER[nz // PAIR:]

    inject(KF, ZERO)

    @pl.loop(0, rep.shape[0])
    def _(i):
        rep[i] = jnp.zeros(rep.shape[1:], F32)

    @pl.loop(0, PAD)
    def _(i):
        maskx[i] = jnp.zeros(maskx.shape[1:], F32)
        maskx[PAD + n_unit + i] = jnp.zeros(maskx.shape[1:], F32)
    gbacc[...] = jnp.zeros_like(gbacc)

    @pl.loop(0, hid // BIG)
    def _(i):
        gw[pl.ds(pl.multiple_of(i * BIG, BIG), BIG), :] = jnp.zeros((BIG, v_chip), F32)

    load_m.wait()
    for cp in send_m:
        cp.wait()
    send_w = remote(w_ref, wbuf.at[:, my_cols], w_sem.at[0], w_sem.at[1], sib)
    send_w.start()
    send_b = remote(b_ref, bias.at[:, my_cols], bias_sem.at[0], bias_sem.at[1], sib)
    send_b.start()

    in_row = LANE // UT
    for s in range(nz):
        for i in WAYS:
            for r in range(n_unit // in_row):
                tile = jnp.broadcast_to(msgs[PAIR * chip_of(s) + i, c, r:r + 1, :], (LANE, LANE)).T
                for t in range(in_row):
                    at = pos[s] * br + i * UT
                    maskx[PAD + r * in_row + t, at:at + UT, :] = tile[t * UT:(t + 1) * UT, :]

    relay(KF, ZERO, 1)
    injected(KF, ZERO)
    load_w.wait()
    load_b.wait()
    send_w.wait()
    send_b.wait()

    def pages(j, k):
        after = {d: (j - d + PAD) // per_row for d in set(k)}
        return [after[k[s]] for s in range(nz)]

    def mask_rows(j, k, slots):
        return jnp.concatenate([maskx[j - k[s] + PAD, block(s), :] for s in slots], axis=0)

    def fwd_group(j, b, g, k0, k1):
        slots = (near, far)[g]
        page = pages(j, KF)

        @functools.partial(lax.fori_loop, k0, k1, init_val=None, unroll=UNROLL)
        def _(k, _):
            at = pl.ds(pl.multiple_of(k * CH, CH), CH)
            logits = jnp.dot(xbuf[b, g * half:(g + 1) * half], wbuf[:, at], preferred_element_type=F32)
            for t in range(CH // LANE):
                at = pl.ds(pl.multiple_of(k * CH + t * LANE, LANE), LANE)
                zt = logits[:, t * LANE:(t + 1) * LANE] + bias[:, at]
                act = jnp.log(1.0 + jnp.maximum(zt, 0.0)) * mask_rows(j, KF, slots)
                for i, s in enumerate(slots):
                    for u in WAYS:
                        r0 = i * br + u * UT
                        row_sum = jnp.sum(act[r0:r0 + UT, :], axis=0, keepdims=True)
                        rep[page[s], PAIR * s + u:PAIR * s + u + 1, at] = rep[page[s], PAIR * s + u:PAIR * s + u + 1, at] + row_sum

    def cut(eighths):
        return n_chunk * eighths // SUB

    fwd_end = n_unit + KF[MAXD]

    def release_far(j):
        @pl.when(j >= 1)
        def _():
            release(KF, j, far)

    @pl.loop(1, fwd_end)
    def _(j):
        b = par(j)
        release_far(j - 1)
        inject(KF, j)
        take_own(KF, j - KF[0])
        arrive(KF, j - KF[0], 0, 0)
        fwd_group(j, b, 0, 0, cut(6))
        relay(KF, j - 2, 3)
        fwd_group(j, b, 0, cut(6), n_chunk)
        release(KF, j, near)
        relay(KF, j - 1, 2)
        relay(KF, j - 3, 4)
        fwd_group(j, b, 1, 0, cut(4))
        relay(KF, j, 1)
        fwd_group(j, b, 1, cut(4), n_chunk)
        injected(KF, j)

        @pl.when(j <= v_chip // 256)
        def _():
            for u in WAYS:
                at = pl.ds(pl.multiple_of((j - 1) * 256 + u * LANE, LANE), LANE)
                wt[at, :] = wbuf[:, at].T

    release_far(jnp.int32(fwd_end - 1))

    for s in range(nz):
        for way, dist in lanes_of(s):
            give_credit(way, dist, 2 if dist < MAXD else 1)

    q_total = q_rows * n_group
    d_total = d_rows * n_group
    v_total = v_loc * n_group
    tau = q_len * math.sqrt(v_total * d_len) / 16.0
    lam_q = 4.0 / (v_total * q_len * q_len)
    lam_d = 4.0 / (v_total * d_len * d_len)
    nd = d_rows // PAIR * n_group
    nq = q_rows // PAIR * n_group
    q0 = PAD // per_row
    d0 = q0 + n_qpage

    @pl.loop(0, n_chunk)
    def _(k):
        at = pl.ds(pl.multiple_of(k * CH, CH), CH)
        for r in range(d_rows // PAIR):
            rdx[c, r * n_group:(r + 1) * n_group, at] = sum(rep[d0 + r * pieces + i, :, at] for i in range(pieces))
        q_sum = sum(rep[q0 + i, :, at] for i in range(n_qpage))
        rdx[c, nd:nd + SUB, at] = sum(q_sum[i * SUB:(i + 1) * SUB] for i in range(n_group // SUB))

    def to_sib(src, dst, i):
        return remote(src, dst, pair_sem.at[i, 0], pair_sem.at[i, 1], sib)

    send_rd = to_sib(rdx.at[c], rdx.at[c], 0)
    send_rd.start()
    inject(KB, ZERO, BWD)
    send_rd.wait()

    def d_reps(at):
        return jnp.concatenate([rdx[0, 0:nd, at], rdx[1, 0:nd, at]], axis=0)

    def q_mean_of(at):
        return jnp.sum(rdx[0, nd:nd + SUB, at] + rdx[1, nd:nd + SUB, at], axis=0, keepdims=True) * (1.0 / q_total)

    def d_mean_of(at):
        return jnp.sum(d_reps(at), axis=0, keepdims=True) * (1.0 / d_total)

    def lanes(v):
        return sum(v[:, t * LANE:(t + 1) * LANE] for t in range(CH // LANE))

    def score_chunk(k, carry):
        s_acc, rq, rd = carry
        at = pl.ds(pl.multiple_of(k * CH, CH), CH)
        q_rep = rep[q0:q0 + n_qpage, :, at].reshape(nq, CH)
        s_acc = s_acc + lax.dot_general(d_reps(at), q_rep, (((1,), (1,)), ((), ())), precision=HIGHEST,
                                        preferred_element_type=F32)
        qm, dm = q_mean_of(at), d_mean_of(at)
        return s_acc, rq + lanes(qm * qm), rd + lanes(dm * dm)

    score, reg_q, reg_d = lax.fori_loop(0, n_chunk, score_chunk,
                                        (jnp.zeros((PAIR * nd, nq), F32), jnp.zeros((1, LANE), F32), jnp.zeros((1, LANE), F32)))

    def turn(n):
        i = lax.broadcasted_iota(jnp.int32, (n, n), 0)
        k = lax.broadcasted_iota(jnp.int32, (n, n), 1)
        same = (i // n_group == k // n_group) & (i % 2 == k % 2)
        return (same & (((i // PAIR) % nz + (k // PAIR) % nz) % nz == z)).astype(F32)

    def exact(a, b):
        return jnp.dot(a, b, precision=HIGHEST, preferred_element_type=F32)

    turn_d, turn_q = turn(PAIR * nd), turn(nq)
    smsg[0, 0:PAIR * nd, 0:nq] = exact(exact(turn_d, score), turn_q)
    smsg[0, PAIR * nd:PAIR * nd + 1, :] = reg_q
    smsg[0, PAIR * nd + 1:PAIR * nd + 2, :] = reg_d
    send_s = [remote(smsg.at[0], smsg.at[t], sm_send.at[t], sm_recv.at[t], peers[t - 1]) for t in range(1, nz)]
    for cp in send_s:
        cp.start()

    pos_rows = jnp.concatenate([msgs[i, 0, 3:4, :] for i in range(n_group)], axis=0)
    spread = (lax.broadcasted_iota(jnp.int32, (LANE, nq), 0)
              == PAIR * (lax.broadcasted_iota(jnp.int32, (LANE, nq), 1) // n_group) + c).astype(F32)
    pos_all = exact(pos_rows, spread)
    pick = (lax.broadcasted_iota(jnp.int32, (n_group, nq), 1) % n_group
            == lax.broadcasted_iota(jnp.int32, (n_group, nq), 0))
    pos_row = jnp.sum(jnp.where(pick, pos_all, 0.0), axis=0, keepdims=True)
    ridx = lax.broadcasted_iota(jnp.int32, (PAIR * nd, nq), 0)
    doc = (ridx % n_group) * d_rows + PAIR * ((ridx % nd) // n_group) + ridx // nd
    target = (doc.astype(F32) == pos_row).astype(F32)

    relay(KB, ZERO, 1, BWD)
    injected(KB, ZERO)
    for cp in send_s:
        cp.wait()
    total = smsg[0]
    for t in range(1, nz):
        total = total + smsg[t]
    scores = total[0:PAIR * nd, 0:nq] * (1.0 / tau)
    top = jnp.max(scores, axis=0, keepdims=True)
    log_norm = top + jnp.log(jnp.sum(jnp.exp(scores - top), axis=0, keepdims=True))
    row_loss = log_norm - jnp.sum(scores * target, axis=0, keepdims=True)
    loss_part = jnp.sum(row_loss, axis=1, keepdims=True)
    gt = (jnp.exp(scores - log_norm) - target) * (1.0 / (q_total * tau))
    gt = exact(exact(turn_d, gt), turn_q)
    g = gt.T
    lossx[c] = jnp.broadcast_to(loss_part, (SUB, LANE))
    send_l = to_sib(lossx.at[c], lossx.at[c], 1)
    send_l.start()
    inject(KB, ZERO + 1, BWD)
    relay(KB, ZERO, 2, BWD)

    @pl.loop(0, n_chunk)
    def _(k):
        at = pl.ds(pl.multiple_of(k * CH, CH), CH)
        q_rep = rep[q0:q0 + n_qpage, :, at].reshape(nq, CH)
        dp = exact(gt, q_rep)
        ddx[0, :, at] = dp[0:nd]
        ddx[1, :, at] = dp[nd:PAIR * nd]
        gq = exact(g, d_reps(at)) + q_mean_of(at) * (2.0 * lam_q / q_total)
        rep[q0:q0 + n_qpage, :, at] = gq.reshape(n_qpage, n_group, CH)

    send_dd = to_sib(ddx.at[o], ddr, 2)
    send_dd.start()
    send_l.wait()
    reg = (jnp.sum(total[PAIR * nd:PAIR * nd + 1, :], axis=1, keepdims=True) * lam_q
           + jnp.sum(total[PAIR * nd + 1:PAIR * nd + 2, :], axis=1, keepdims=True) * lam_d)
    lossf[0] = (lossx[0] + lossx[1]) * (1.0 / q_total) + reg

    send_loss = [remote(lossf.at[0], lossf.at[1], loss_send.at[t], loss_recv, peers[t - 1]) for t in range(1, nz)]

    @pl.when(z == 0)
    def _():
        for cp in send_loss:
            cp.start()
    relay(KB, ZERO + 1, 1, BWD)
    injected(KB, ZERO + 1)
    relay(KB, ZERO, 3, BWD)
    send_dd.wait()

    @pl.loop(0, n_chunk)
    def _(k):
        at = pl.ds(pl.multiple_of(k * CH, CH), CH)
        gd = ddx[c, :, at] + ddr[:, at] + d_mean_of(at) * (2.0 * lam_d / d_total)
        for r in range(d_rows // PAIR):
            for i in range(pieces):
                rep[d0 + r * pieces + i, :, at] = gd[r * n_group:(r + 1) * n_group]

    def bwd_chunk(j, b, page, k):
        cols = pl.ds(pl.multiple_of(k * CH, CH), CH)
        logits = jnp.dot(xbuf[b], wbuf[:, cols], preferred_element_type=F32)
        low = []
        for t in range(CH // LANE):
            at = pl.ds(pl.multiple_of(k * CH + t * LANE, LANE), LANE)
            zt = logits[:, t * LANE:(t + 1) * LANE] + bias[:, at]
            grad = jnp.concatenate([jnp.broadcast_to(rep[page[s], PAIR * s + u:PAIR * s + u + 1, at], (UT, LANE))
                                    for s in ORDER for u in WAYS], axis=0)
            gz = jnp.where(zt > 0.0, grad * mask_rows(j, KB, ORDER) / (1.0 + jnp.maximum(zt, 0.0)), 0.0)
            gbacc[:, at] = gbacc[:, at] + jnp.sum(gz.reshape(rows // SUB, SUB, LANE), axis=0)
            low.append(gz.astype(BF16))
        low = jnp.concatenate(low, axis=1)
        gbuf[:, cols] = low
        gw[:, cols] = gw[:, cols] + jnp.dot(xt[...], low, preferred_element_type=F32)

    def bwd_hidden(k0, k1):
        wide = hid // 4

        @functools.partial(lax.fori_loop, k0, k1, init_val=None, unroll=UNROLL)
        def _(k, _):
            cols = pl.ds(pl.multiple_of(k * wide, wide), wide)
            pbuf[:, cols] = jnp.dot(gbuf[...], wt[:, cols], preferred_element_type=F32).astype(BF16)

    def deep(n):
        return lax.rem(n + BIG, DEEP)

    def rs_copy(n, way, dist):
        return remote(sbuf.at[way, dist - 1], rbuf.at[way, dist - 2, deep(n)], rs_send.at[way, dist - 1],
                      rs_recv.at[way, dist - 2, deep(n)], dev(behind[way], c))

    def home_copy(n, way, cc, i):
        return remote(sbuf.at[way, 0, pl.ds(i * UT, UT)], hbuf.at[way, cc, deep(n)], h_send.at[way, i],
                      h_recv.at[way, cc, deep(n)], dev(behind[way], i))

    def pair_copy(n):
        return remote(sst.at[par(n)], sibp.at[par(n)], sp_send.at[par(n)], sp_recv.at[par(n)], sib)

    def rs_sent(n, way, dist):
        @pl.when(carries(way, dist, n))
        def _():
            if dist == 1:
                for i in WAYS:
                    home_copy(n, way, c, i).wait_send()
            else:
                rs_copy(n, way, dist).wait_send()

    def rs_go(n, way, dist):
        @pl.when(n >= DEEP)
        def _():
            if dist == 1:
                for i in WAYS:
                    pl.semaphore_wait(h_cred.at[way, i])
            else:
                pl.semaphore_wait(rs_cred.at[way, dist - 1])
        if dist == 1:
            for i in WAYS:
                home_copy(n, way, c, i).start()
        else:
            rs_copy(n, way, dist).start()

    def rs_event(n, way, dist):
        s = slot(way, dist)
        rs_sent(n - (2 if dist == MAXD else 1), way, dist)
        mine = (lambda: pbuf[block(s), :]) if dist == MAXD else (lambda: part[s, deep(n)])
        incoming = carries(way, dist + 1, n) if dist + 1 <= MAXD else None
        if dist == MAXD:
            alone, joined = carries(way, dist, n), None
        elif dist + 1 == MAXD:
            alone, joined = carries(way, dist, n) & (par(n) != way), incoming
        else:
            alone, joined = None, incoming
        if alone is not None:
            @pl.when(alone)
            def _():
                sbuf[way, dist - 1] = mine()
                rs_go(n, way, dist)
        if joined is not None:
            @pl.when(joined)
            def _():
                rs_copy(n, way, dist + 1).wait_recv()
                got = rbuf[way, dist - 1, deep(n)]
                sbuf[way, dist - 1] = (mine().astype(F32) + got.astype(F32)).astype(BF16)

                @pl.when(n + DEEP < n_unit)
                def _():
                    pl.semaphore_signal(rs_cred.at[way, dist], device_id=dev(ahead[way], c), device_id_type=MESH)
                rs_go(n, way, dist)

    def rs_home(n):
        @pl.when((n >= 0) & (n < n_unit))
        def _():
            for cc in WAYS:
                for way in WAYS:
                    home_copy(n, way, cc, 0).wait_recv()
                at = unit_rows(n)
                acc_h[cc, n // per_row, at] = (acc_h[cc, n // per_row, at].astype(F32) + hbuf[0, cc, deep(n)].astype(F32)
                                               + hbuf[1, cc, deep(n)].astype(F32)).astype(BF16)

                @pl.when(n + DEEP < n_unit)
                def _():
                    for way in WAYS:
                        pl.semaphore_signal(h_cred.at[way, c], device_id=dev(ahead[way], cc), device_id_type=MESH)

    def pair_send(n):
        @pl.when((n >= 2) & (n < n_unit + 2))
        def _():
            pair_copy(n - 2).wait_send()

        @pl.when((n >= 0) & (n < n_unit))
        def _():
            sst[par(n)] = pbuf[part_of_block(0, o), :]

            @pl.when(n >= 2)
            def _():
                pl.semaphore_wait(sp_cred)
            pair_copy(n).start()
            acc_h[c, n // per_row, unit_rows(n)] = pbuf[part_of_block(0, c), :]

    def pair_take(n):
        @pl.when((n >= 0) & (n < n_unit))
        def _():
            pair_copy(n).wait_recv()
            acc_h[o, n // per_row, unit_rows(n)] = sibp[par(n)]

            @pl.when(n + 2 < n_unit)
            def _():
                pl.semaphore_signal(sp_cred, device_id=sib, device_id_type=MESH)

    last = n_unit + KB[MAXD]

    def rs_both(n, dist):
        for way in WAYS:
            rs_event(n, way, dist)

    @pl.loop(1, last)
    def _(j):
        b = par(j)
        page = pages(j, KB)

        def weights(k0, k1):
            @functools.partial(lax.fori_loop, k0, k1, init_val=None, unroll=UNROLL)
            def _(k, _):
                bwd_chunk(j, b, page, k)

        relay(KB, j - 2, 4)
        take_own(KB, j - 1)
        arrive(KB, j - 1, 0, 0)
        rs_both(j - 3, 4)
        rs_both(j - 5, 1)
        xt[...] = xbuf[b].T
        weights(0, cut(4))

        @pl.when(j >= 2)
        def _():
            relay(KB, j, 1, BWD)
        rs_both(j - 4, 2)
        weights(cut(4), cut(6))

        @pl.when(j >= 2)
        def _():
            relay(KB, j - 1, 3, BWD)
        weights(cut(6), n_chunk)
        release(KB, j, ORDER)
        rs_both(j - 3, 3)
        bwd_hidden(0, 3)

        @pl.when(j >= 2)
        def _():
            injected(KB, j)
        inject(KB, j + 1, BWD)
        relay(KB, j, 2, BWD)
        rs_home(j - 5)
        bwd_hidden(3, 4)
        for s in range(1, nz):
            if s != MAXD:
                part[s, deep(j - KB[s])] = pbuf[block(s), :]
        pair_send(j - 1)
        pair_take(j - 2)

    n_part = gx_send.shape[0] - 1
    step = v_loc // n_part
    send_g = []
    for k in range(n_part):
        theirs = pl.ds(pl.multiple_of(o * v_loc + k * step, step), step)
        send_g.append(remote(gw.at[:, theirs], grecv.at[:, pl.ds(k * step, step)], gx_send.at[k], gx_recv.at[k], sib))
    send_gb = remote(gbacc.at[:, sib_cols], gbrecv, gx_send.at[n_part], gx_recv.at[n_part], sib)
    for cp in send_g:
        cp.start()
    send_gb.start()

    @pl.loop(last, n_unit + 5)
    def _(j):
        rs_both(j - 3, 4)
        rs_both(j - 5, 1)
        rs_both(j - 4, 2)
        rs_both(j - 3, 3)
        pair_send(j - 1)
        rs_home(j - 5)
    for way in WAYS:
        rs_sent(jnp.int32(n_unit - 1), way, 1)

    outs = []
    for cc in WAYS:
        outs.append(pltpu.make_async_copy(acc_h.at[cc, pl.ds(0, n_qpage)], dq_out.at[:, cc], out_sem.at[len(outs)]))
        for r in range(d_rows // PAIR):
            outs.append(pltpu.make_async_copy(acc_h.at[cc, pl.ds(n_qpage + r * pieces, pieces)], dd_out.at[r, cc],
                                              out_sem.at[len(outs)]))
    for cp in outs:
        cp.start()
    for k in range(n_part):
        send_g[k].wait_recv()
        at = pl.ds(pl.multiple_of(c * v_loc + k * step, step), step)

        @pl.loop(0, hid // BIG)
        def _(i):
            rr = pl.ds(pl.multiple_of(i * BIG, BIG), BIG)
            wbuf[rr, at] = (gw[rr, at] + grecv[rr, pl.ds(k * step, step)]).astype(BF16)
        outs.append(pltpu.make_async_copy(wbuf.at[:, at], gw_out.at[:, pl.ds(k * step, step)], out_sem.at[len(outs)]))
        outs[-1].start()
    send_gb.wait_recv()
    gb_ref[...] = jnp.sum(gbacc[:, my_cols] + gbrecv[...], axis=0, keepdims=True)

    @pl.when(z == 0)
    def _():
        for cp in send_loss:
            cp.wait_send()
        loss_ref[...] = lossf[0]

    @pl.when(z != 0)
    def _():
        send_loss[0].wait_recv()
        loss_ref[...] = lossf[1]
    for cp in send_g:
        cp.wait_send()
    send_gb.wait_send()
    for cp in outs:
        cp.wait()


def solution(mesh):
    n_group = mesh.shape['tp']
    nz = n_group // PAIR
    row_spec = P(('dp', 'tp'))
    mask_spec = P(('dp', 'tp'), None)
    hid_spec = P(('dp', 'tp'), None, None)

    def local_step(q_hidden, d_hidden, q_mask, d_mask, positive, w_head, b_head):
        q_rows, q_len, hid = q_hidden.shape
        d_rows, d_len, _ = d_hidden.shape
        v_loc = w_head.shape[1]
        v_chip = PAIR * v_loc
        per_row = q_len // UT
        pieces = d_len // q_len
        n_page = q_rows // PAIR + d_rows // PAIR * pieces
        n_unit = n_page * per_row
        rows = nz * PAIR * UT
        nd, nq = d_rows // PAIR * n_group, q_rows // PAIR * n_group
        by_core = jnp.concatenate([jnp.swapaxes(q_mask.reshape(q_rows // PAIR, 2, q_len), 0, 1).reshape(2, -1),
                                   jnp.swapaxes(d_mask.reshape(d_rows // PAIR, 2, d_len), 0, 1).reshape(2, -1)], axis=1)
        by_core = by_core.astype(F32).reshape(2, -1, LANE)
        by_core = jnp.pad(by_core, ((0, 0), (0, 3 - by_core.shape[1]), (0, 0)))
        where = jnp.pad(positive.astype(F32), (0, LANE - q_rows)).reshape(1, 1, LANE)
        msg = jnp.concatenate([by_core, jnp.broadcast_to(where, (2, 1, LANE))], axis=1)
        s_rows = -(-(PAIR * nd + 2) // SUB) * SUB
        n_part = 4 if v_loc >= 512 else 2
        n_load = PAIR * (1 + d_rows // PAIR)
        dma, reg = pltpu.SemaphoreType.DMA, pltpu.SemaphoreType.REGULAR
        anym = pl.BlockSpec(memory_space=pl.ANY)
        vm = pl.BlockSpec(memory_space=pltpu.VMEM)
        q_shape = (q_rows // PAIR, 2, q_len, hid)
        d_shape = (d_rows // PAIR, 2, pieces, q_len, hid)
        out_shape = (
            jax.ShapeDtypeStruct((SUB, LANE), F32),
            jax.ShapeDtypeStruct((hid, v_loc), BF16),
            jax.ShapeDtypeStruct((1, v_loc), F32),
            jax.ShapeDtypeStruct(q_shape, BF16),
            jax.ShapeDtypeStruct(d_shape, BF16),
        )
        scratch = [
            pltpu.VMEM((hid, v_chip), BF16),
            pltpu.VMEM((v_chip, hid), BF16),
            pltpu.VMEM((hid, v_chip), F32),
            pltpu.VMEM((hid, v_loc), F32),
            pltpu.VMEM(((n_unit + PAIR * PAD) // per_row, n_group, v_chip), F32),
            pltpu.VMEM((n_unit + PAIR * PAD, rows, LANE), F32),
            pltpu.VMEM((PAIR, n_page, q_len, hid), BF16),
            pltpu.VMEM((PAIR, n_page, q_len, hid), BF16),
            pltpu.VMEM((nz, DEEP, PAIR * UT, hid), BF16),
            pltpu.VMEM((PAIR, rows, hid), BF16),
            pltpu.VMEM((PAIR, MAXD - 1, DEEP, PAIR * UT, hid), BF16),
            pltpu.VMEM((PAIR, MAXD, PAIR * UT, hid), BF16),
            pltpu.VMEM((PAIR, 2, DEEP, UT, hid), BF16),
            pltpu.VMEM((PAIR, UT, hid), BF16),
            pltpu.VMEM((PAIR, UT, hid), BF16),
            pltpu.VMEM((rows, v_chip), BF16),
            pltpu.VMEM((rows, hid), BF16),
            pltpu.VMEM((hid, rows), BF16),
            pltpu.VMEM((PAIR, nd + SUB, v_chip), F32),
            pltpu.VMEM((PAIR, nd, v_chip), F32),
            pltpu.VMEM((nd, v_chip), F32),
            pltpu.VMEM((1, v_chip), F32),
            pltpu.VMEM((SUB, v_chip), F32),
            pltpu.VMEM((SUB, v_loc), F32),
            pltpu.VMEM((n_group, 2, 4, LANE), F32),
            pltpu.VMEM((nz, s_rows, LANE), F32),
            pltpu.VMEM((PAIR, SUB, LANE), F32),
            pltpu.VMEM((PAIR, SUB, LANE), F32),
            dma((PAIR, MAXD, 2)), dma((PAIR, nz, 2)), reg((PAIR, MAXD)), dma((PAIR, 2)), reg((PAIR, 2)), dma, reg,
            dma((PAIR, MAXD)), dma((PAIR, MAXD - 1, DEEP)), reg((PAIR, MAXD)), dma((PAIR, 2)), dma((PAIR, 2, DEEP)), reg((PAIR, 2)),
            dma((PAIR,)), dma((PAIR,)), reg,
            dma((n_load + 3,)), dma((PAIR,)), dma((PAIR,)), dma((n_group - 1,)), dma((n_group - 1,)), dma((nz,)), dma((nz,)),
            dma((3, 2)), dma((n_part + 1,)), dma((n_part + 1,)), dma((nz,)), dma, dma((n_load + n_part,)),
        ]
        loss, gw, gb, dq, dd = pl.pallas_call(
            functools.partial(kernel, n_group, q_rows, q_len, d_rows, d_len),
            out_shape=out_shape,
            in_specs=[anym] * 5,
            out_specs=(vm, anym, vm, anym, anym),
            scratch_shapes=scratch,
            compiler_params=pltpu.CompilerParams(collective_id=0, has_side_effects=True, vmem_limit_bytes=67043328),
        )(q_hidden.reshape(q_shape), d_hidden.reshape(d_shape), w_head, b_head.reshape(1, v_loc), msg)
        return (loss[0, 0:1], gw, gb.reshape(v_loc), dq.reshape(q_hidden.shape), dd.reshape(d_hidden.shape))

    return jax.shard_map(local_step, mesh=mesh,
                         in_specs=(hid_spec, hid_spec, mask_spec, mask_spec, row_spec, P(None, 'tp'), P('tp')),
                         out_specs=(P('dp'), P('dp', 'tp'), row_spec, hid_spec, hid_spec),
                         check_vma=False)
```

time: 2890 us -> 499 us (0.17)
  waiting for transfers between devices: 2000 us -> 0 us
  matrix products: 562 us -> 0 us
  Pallas kernels: 0 us -> 486 us
  local copies, waits for them, and re-layouts: 147 us -> 9.27 us
  blocking collectives: 94.5 us -> 0 us
  other arithmetic: 53.1 us -> 1.94 us
    all_gather x36 -> x0, waiting for transfers between devices: 1320 us -> none  [one_row(): gathered = lax.all_gather(hid_row, 'tp')]
    reduce_scatter x18 -> x0, waiting for transfers between devices: 679 us -> none  [one_row(): own_hid = lax.psum_scatter(part_hid, 'tp', scatter_dimension=0, tiled=True)]
    dot_general x75 -> x0, matrix products: 562 us -> none  [the longest x36 251 us: head_logits(): jnp.einsum('pld,dv->plv', gathered, w_head, preferred_element_type=jnp.fl...]
    pallas_call x0 -> x1, Pallas kernels: none -> 486 us  [local_step(): pl.pallas_call(functools.partial(kernel, n_group, q_rows, q_len, d_rows,...]
    dynamic_slice x36 -> x0, local copies, waits for them, and re-layouts: 50.2 us -> none  [side_reps(): row_reps = lax.map(one_row, (hidden, jnp.swapaxes(mask_all, 0, 1)))]
    psum x1 -> x0, blocking collectives: 44.3 us -> none  [local_step(): score_sum, reg_sum = lax.psum((score_part, reg_part), 'tp')]
    reduce_sum x22 -> x0, other arithmetic: 43.4 us -> none  [the longest x18 41 us: one_row(): acc_b = acc_b + jnp.sum(grad_logits, axis=(0, 1))]
    while x83 -> x0, local copies, waits for them, and re-layouts: 40.8 us -> none
  transfers between devices with their start and end apart: 54 -> 0, of which waited for: 54 -> 0; matrix products, arithmetic and copies ran while one was open for 9% -> 0% of each run, Pallas kernels for 0% -> 0%
where the time goes in v2:
time: 499 us; the launch traced here: 498 us
  Pallas kernels  486 us (97%)
  local copies, waits for them, and re-layouts  9.27 us (2%)
    pallas_call x1, Pallas kernels, local_step(): pl.pallas_call(functools.partial(kernel, n_group, q_rows, q_len, d_rows,...  486 us

profile of v2, /device:TPU:21, one launch (start us, length us, event | category | flops | bytes accessed | tf_op | source)
XLA Modules:
  0.0 498.3 jit_solution(10989191413365615761)
XLA Ops:
  0.6 0.7 convert_element_type.14
  1.3 0.7 copy.13
  2.0 0.1 reshape.45
  2.1 0.7 add_convert_fusion
  2.8 0.6 pad_maximum_fusion.msg_ref
  3.4 486.5 %shard_map.110 = (f32[8,128]{1,0:T(8,128)}, bf16[1024,2048]{1,0:T(8,128)(2,1)}, f32[1,2048]{1,0:T(1,128)}, bf16[8,2,32,1024]{3,2,1,0:T(8,128)(2,1)}, bf16[1,2,4,32,1024]{4,3,2,1,0:T(8,128)(2,1)}) custom-call(bf16[8,2,32,1024]{3,2,1,0:T(8,128)(2,1)} %bitcast.10, bf16[1,2,4,32,1024]{4,3,2,1,0:T(8,128)(2,1)} %bitcast.12, bf16[1024,2048]{1,0:T(8,128)(2,1)} %w_ref.1, ...), custom_call_target="tpu_custom_call" | custom-call | tf_op jit(solution)/shard_map/pallas_call | solution.py:788
  489.9 1.2 slice.3
  491.1 0.0 copy-start.2
  491.1 0.0 copy-start
  491.1 0.0 copy-start.1
  491.1 4.9 copy.18
  496.0 0.0 copy-done.2
  496.0 0.6 copy.19
  496.6 0.0 copy-done
  496.6 1.0 copy.20
  497.5 0.0 copy-done.1
  497.6 0.8 copy.21
  (3 shorter events, 0.0 us)
Async XLA Ops:
  491.1 4.9 copy-start.2
  491.1 5.5 %copy-start = (bf16[8,2,32,1024]{3,2,1,0:T(8,128)(2,1)S(1)}, bf16[8,2,32,1024]{3,2,1,0:T(8,128)(2,1)}, u32[]{:S(2)}) copy-start(bf16[8,2,32,1024]{3,2,1,0:T(8,128)(2,1)} %get-tuple-element.13) | copy-start | bytes 3145732
  491.1 6.5 %copy-start.1 = (bf16[1,2,4,32,1024]{4,3,2,1,0:T(8,128)(2,1)S(1)}, bf16[1,2,4,32,1024]{4,3,2,1,0:T(8,128)(2,1)}, u32[]{:S(2)}) copy-start(bf16[1,2,4,32,1024]{4,3,2,1,0:T(8,128)(2,1)} %get-tuple-element.14) | copy-start | bytes 1572868

commit v3 on v2

--- a/solution.py
+++ b/solution.py
@@ -15,6 +15,7 @@
 
 UT = 16
 CH = 512
+CB = 1024
 MAXD = 4
 KF = (1, 1, 2, 2, 3, 2, 1, 1)
 KB = (1, 1, 1, 2, 2, 2, 1, 1)
@@ -32,7 +33,7 @@
            rdx, ddx, ddr, bias, gbacc, gbrecv, msgs, smsg, lossx, lossf,
            ag_send, ag_recv, ag_cred, inj_send, inj_cred, sib_send, sib_cred,
            rs_send, rs_recv, rs_cred, h_send, h_recv, h_cred, sp_send, sp_recv, sp_cred,
-           loc_sem, w_sem, bias_sem, msg_send, msg_recv, sm_send, sm_recv, pair_sem, gx_send, gx_recv,
+           loc_sem, w_sem, bias_sem, msg_send, msg_recv, sm_send, sm_recv, pair_sem, gx_send, gx_recv, gx_cred,
            loss_send, loss_recv, out_sem):
     ZERO = jnp.int32(0)
     nz = n_group // PAIR
@@ -115,6 +116,10 @@
     send_m = [remote(msg_ref, msgs.at[me], msg_send.at[k], msg_recv.at[k], d) for k, d in enumerate(others)]
     for cp in send_m:
         cp.start()
+    send_w = remote(w_ref, wbuf.at[:, my_cols], w_sem.at[0], w_sem.at[1], sib)
+    send_w.start()
+    send_b = remote(b_ref, bias.at[:, my_cols], bias_sem.at[0], bias_sem.at[1], sib)
+    send_b.start()
     for cp in loads:
         cp.wait()
 
@@ -249,10 +254,6 @@
     load_m.wait()
     for cp in send_m:
         cp.wait()
-    send_w = remote(w_ref, wbuf.at[:, my_cols], w_sem.at[0], w_sem.at[1], sib)
-    send_w.start()
-    send_b = remote(b_ref, bias.at[:, my_cols], bias_sem.at[0], bias_sem.at[1], sib)
-    send_b.start()
 
     in_row = LANE // UT
     for s in range(nz):
@@ -442,11 +443,16 @@
         dp = exact(gt, q_rep)
         ddx[0, :, at] = dp[0:nd]
         ddx[1, :, at] = dp[nd:PAIR * nd]
+
+    send_dd = to_sib(ddx.at[o], ddr, 2)
+    send_dd.start()
+
+    @pl.loop(0, n_chunk)
+    def _(k):
+        at = pl.ds(pl.multiple_of(k * CH, CH), CH)
         gq = exact(g, d_reps(at)) + q_mean_of(at) * (2.0 * lam_q / q_total)
         rep[q0:q0 + n_qpage, :, at] = gq.reshape(n_qpage, n_group, CH)
 
-    send_dd = to_sib(ddx.at[o], ddr, 2)
-    send_dd.start()
     send_l.wait()
     reg = (jnp.sum(total[PAIR * nd:PAIR * nd + 1, :], axis=1, keepdims=True) * lam_q
            + jnp.sum(total[PAIR * nd + 1:PAIR * nd + 2, :], axis=1, keepdims=True) * lam_d)
@@ -472,11 +478,11 @@
                 rep[d0 + r * pieces + i, :, at] = gd[r * n_group:(r + 1) * n_group]
 
     def bwd_chunk(j, b, page, k):
-        cols = pl.ds(pl.multiple_of(k * CH, CH), CH)
+        cols = pl.ds(pl.multiple_of(k * CB, CB), CB)
         logits = jnp.dot(xbuf[b], wbuf[:, cols], preferred_element_type=F32)
         low = []
-        for t in range(CH // LANE):
-            at = pl.ds(pl.multiple_of(k * CH + t * LANE, LANE), LANE)
+        for t in range(CB // LANE):
+            at = pl.ds(pl.multiple_of(k * CB + t * LANE, LANE), LANE)
             zt = logits[:, t * LANE:(t + 1) * LANE] + bias[:, at]
             grad = jnp.concatenate([jnp.broadcast_to(rep[page[s], PAIR * s + u:PAIR * s + u + 1, at], (UT, LANE))
                                     for s in ORDER for u in WAYS], axis=0)
@@ -602,6 +608,9 @@
 
     last = n_unit + KB[MAXD]
 
+    def part_b(eighths):
+        return v_chip // CB * eighths // SUB
+
     def rs_both(n, dist):
         for way in WAYS:
             rs_event(n, way, dist)
@@ -622,18 +631,18 @@
         rs_both(j - 3, 4)
         rs_both(j - 5, 1)
         xt[...] = xbuf[b].T
-        weights(0, cut(4))
+        weights(0, part_b(4))
 
         @pl.when(j >= 2)
         def _():
             relay(KB, j, 1, BWD)
         rs_both(j - 4, 2)
-        weights(cut(4), cut(6))
+        weights(part_b(4), part_b(6))
 
         @pl.when(j >= 2)
         def _():
             relay(KB, j - 1, 3, BWD)
-        weights(cut(6), n_chunk)
+        weights(part_b(6), v_chip // CB)
         release(KB, j, ORDER)
         rs_both(j - 3, 3)
         bwd_hidden(0, 3)
@@ -656,20 +665,43 @@
     send_g = []
     for k in range(n_part):
         theirs = pl.ds(pl.multiple_of(o * v_loc + k * step, step), step)
-        send_g.append(remote(gw.at[:, theirs], grecv.at[:, pl.ds(k * step, step)], gx_send.at[k], gx_recv.at[k], sib))
+        send_g.append(remote(gw.at[:, theirs], grecv.at[k % PAIR], gx_send.at[k], gx_recv.at[k], sib))
     send_gb = remote(gbacc.at[:, sib_cols], gbrecv, gx_send.at[n_part], gx_recv.at[n_part], sib)
-    for cp in send_g:
+    for cp in send_g[:PAIR]:
         cp.start()
     send_gb.start()
 
-    @pl.loop(last, n_unit + 5)
-    def _(j):
-        rs_both(j - 3, 4)
-        rs_both(j - 5, 1)
-        rs_both(j - 4, 2)
-        rs_both(j - 3, 3)
-        pair_send(j - 1)
-        rs_home(j - 5)
+    w_outs = []
+
+    def add_part():
+        k = len(w_outs)
+        send_g[k].wait_recv()
+        at = pl.ds(pl.multiple_of(c * v_loc + k * step, step), step)
+
+        @pl.loop(0, hid // BIG)
+        def _(i):
+            rr = pl.ds(pl.multiple_of(i * BIG, BIG), BIG)
+            wbuf[rr, at] = (gw[rr, at] + grecv[k % PAIR, rr]).astype(BF16)
+        w_outs.append(pltpu.make_async_copy(wbuf.at[:, at], gw_out.at[:, pl.ds(k * step, step)], out_sem.at[n_load + k]))
+        w_outs[-1].start()
+        if k + PAIR < n_part:
+            pl.semaphore_signal(gx_cred, device_id=sib, device_id_type=MESH)
+            pl.semaphore_wait(gx_cred)
+            send_g[k + PAIR].start()
+
+    n_load = len(loads)
+    for j in range(last, n_unit + 5):
+        n = ZERO + j
+        rs_both(n - 3, 4)
+        rs_both(n - 5, 1)
+        if j > last:
+            add_part()
+        rs_both(n - 4, 2)
+        rs_both(n - 3, 3)
+        pair_send(n - 1)
+        if j == last:
+            add_part()
+        rs_home(n - 5)
     for way in WAYS:
         rs_sent(jnp.int32(n_unit - 1), way, 1)
 
@@ -681,16 +713,8 @@
                                               out_sem.at[len(outs)]))
     for cp in outs:
         cp.start()
-    for k in range(n_part):
-        send_g[k].wait_recv()
-        at = pl.ds(pl.multiple_of(c * v_loc + k * step, step), step)
-
-        @pl.loop(0, hid // BIG)
-        def _(i):
-            rr = pl.ds(pl.multiple_of(i * BIG, BIG), BIG)
-            wbuf[rr, at] = (gw[rr, at] + grecv[rr, pl.ds(k * step, step)]).astype(BF16)
-        outs.append(pltpu.make_async_copy(wbuf.at[:, at], gw_out.at[:, pl.ds(k * step, step)], out_sem.at[len(outs)]))
-        outs[-1].start()
+    while len(w_outs) < n_part:
+        add_part()
     send_gb.wait_recv()
     gb_ref[...] = jnp.sum(gbacc[:, my_cols] + gbrecv[...], axis=0, keepdims=True)
 
@@ -698,16 +722,16 @@
     def _():
         for cp in send_loss:
             cp.wait_send()
-        loss_ref[...] = lossf[0]
+        loss_ref[...] = lossf[0, 0:1, 0:1]
 
     @pl.when(z != 0)
     def _():
         send_loss[0].wait_recv()
-        loss_ref[...] = lossf[1]
+        loss_ref[...] = lossf[1, 0:1, 0:1]
     for cp in send_g:
         cp.wait_send()
     send_gb.wait_send()
-    for cp in outs:
+    for cp in outs + w_outs:
         cp.wait()
 
 
@@ -744,7 +768,7 @@
         q_shape = (q_rows // PAIR, 2, q_len, hid)
         d_shape = (d_rows // PAIR, 2, pieces, q_len, hid)
         out_shape = (
-            jax.ShapeDtypeStruct((SUB, LANE), F32),
+            jax.ShapeDtypeStruct((1, 1), F32),
             jax.ShapeDtypeStruct((hid, v_loc), BF16),
             jax.ShapeDtypeStruct((1, v_loc), F32),
             jax.ShapeDtypeStruct(q_shape, BF16),
@@ -754,7 +778,7 @@
             pltpu.VMEM((hid, v_chip), BF16),
             pltpu.VMEM((v_chip, hid), BF16),
             pltpu.VMEM((hid, v_chip), F32),
-            pltpu.VMEM((hid, v_loc), F32),
+            pltpu.VMEM((PAIR, hid, v_loc // n_part), F32),
             pltpu.VMEM(((n_unit + PAIR * PAD) // per_row, n_group, v_chip), F32),
             pltpu.VMEM((n_unit + PAIR * PAD, rows, LANE), F32),
             pltpu.VMEM((PAIR, n_page, q_len, hid), BF16),
@@ -783,7 +807,7 @@
             dma((PAIR, MAXD)), dma((PAIR, MAXD - 1, DEEP)), reg((PAIR, MAXD)), dma((PAIR, 2)), dma((PAIR, 2, DEEP)), reg((PAIR, 2)),
             dma((PAIR,)), dma((PAIR,)), reg,
             dma((n_load + 3,)), dma((PAIR,)), dma((PAIR,)), dma((n_group - 1,)), dma((n_group - 1,)), dma((nz,)), dma((nz,)),
-            dma((3, 2)), dma((n_part + 1,)), dma((n_part + 1,)), dma((nz,)), dma, dma((n_load + n_part,)),
+            dma((3, 2)), dma((n_part + 1,)), dma((n_part + 1,)), reg, dma((nz,)), dma, dma((n_load + n_part,)),
         ]
         loss, gw, gb, dq, dd = pl.pallas_call(
             functools.partial(kernel, n_group, q_rows, q_len, d_rows, d_len),
@@ -793,7 +817,7 @@
             scratch_shapes=scratch,
             compiler_params=pltpu.CompilerParams(collective_id=0, has_side_effects=True, vmem_limit_bytes=67043328),
         )(q_hidden.reshape(q_shape), d_hidden.reshape(d_shape), w_head, b_head.reshape(1, v_loc), msg)
-        return (loss[0, 0:1], gw, gb.reshape(v_loc), dq.reshape(q_hidden.shape), dd.reshape(d_hidden.shape))
+        return (loss.reshape(1), gw, gb.reshape(v_loc), dq.reshape(q_hidden.shape), dd.reshape(d_hidden.shape))
 
     return jax.shard_map(local_step, mesh=mesh,
                          in_specs=(hid_spec, hid_spec, mask_spec, mask_spec, row_spec, P(None, 'tp'), P('tp')),

time: 499 us -> 473 us (0.948)
  Pallas kernels: 486 us -> 461 us
    pallas_call x1, Pallas kernels: 486 us -> 461 us  [local_step(): pl.pallas_call(functools.partial(kernel, n_group, q_rows, q_len, d_rows,...]
where the time goes in v3:
time: 473 us
  Pallas kernels  461 us (97%)
  local copies, waits for them, and re-layouts  8.09 us (2%)
    pallas_call x1, Pallas kernels, local_step(): pl.pallas_call(functools.partial(kernel, n_group, q_rows, q_len, d_rows,...  461 us

profile of v3, /device:TPU:21, one launch (start us, length us, event | category | flops | bytes accessed | tf_op | source)
XLA Modules:
  0.0 473.0 jit_solution(16806234361899419916)
XLA Ops:
  0.6 0.7 convert_element_type.14
  1.3 0.7 copy.13
  2.0 0.1 reshape.48
  2.1 0.7 add_convert_fusion
  2.8 0.6 pad_maximum_fusion.msg_ref
  3.4 460.6 %shard_map.110 = (f32[1,1]{1,0:T(1,128)}, bf16[1024,2048]{1,0:T(8,128)(2,1)}, f32[1,2048]{1,0:T(1,128)}, bf16[8,2,32,1024]{3,2,1,0:T(8,128)(2,1)}, bf16[1,2,4,32,1024]{4,3,2,1,0:T(8,128)(2,1)}) custom-call(bf16[8,2,32,1024]{3,2,1,0:T(8,128)(2,1)} %bitcast.10, bf16[1,2,4,32,1024]{4,3,2,1,0:T(8,128)(2,1)} %bitcast.12, bf16[1024,2048]{1,0:T(8,128)(2,1)} %w_ref.1, ...), custom_call_target="tpu_custom_call" | custom-call | tf_op jit(solution)/shard_map/pallas_call | solution.py:812
  464.6 0.0 copy-start.2
  464.6 0.0 copy-start
  464.6 0.0 copy-start.1
  464.6 4.9 %copy.20 = bf16[1024,2048]{1,0:T(8,128)(2,1)} copy(bf16[1024,2048]{1,0:T(8,128)(2,1)} %get-tuple-element.21) | data formatting | bytes 8388608
  469.5 0.0 copy-done.2
  469.6 0.6 copy.21
  470.1 0.0 copy-done
  470.2 1.0 copy.22
  471.1 0.0 copy-done.1
  471.1 0.8 copy.23
  (3 shorter events, 0.0 us)
Async XLA Ops:
  464.6 4.9 %copy-start.2 = (f32[1,2048]{1,0:T(1,128)S(1)}, f32[1,2048]{1,0:T(1,128)}, u32[]{:S(2)}) copy-start(f32[1,2048]{1,0:T(1,128)} %get-tuple-element.12) | copy-start | bytes 24580
  464.6 5.5 %copy-start = (bf16[8,2,32,1024]{3,2,1,0:T(8,128)(2,1)S(1)}, bf16[8,2,32,1024]{3,2,1,0:T(8,128)(2,1)}, u32[]{:S(2)}) copy-start(bf16[8,2,32,1024]{3,2,1,0:T(8,128)(2,1)} %get-tuple-element.13) | copy-start | bytes 3145732
  464.6 6.5 %copy-start.1 = (bf16[1,2,4,32,1024]{4,3,2,1,0:T(8,128)(2,1)S(1)}, bf16[1,2,4,32,1024]{4,3,2,1,0:T(8,128)(2,1)}, u32[]{:S(2)}) copy-start(bf16[1,2,4,32,1024]{4,3,2,1,0:T(8,128)(2,1)} %get-tuple-element.14) | copy-start | bytes 1572868

commit v4 on v3

--- a/solution.py
+++ b/solution.py
@@ -27,7 +27,7 @@
 
 
 def kernel(n_group, q_rows, q_len, d_rows, d_len,
-           q_ref, d_ref, w_ref, b_ref, msg_ref,
+           q_ref, d_ref, w_ref, b_ref, qm_ref, dm_ref, pos_ref,
            loss_ref, gw_out, gb_ref, dq_out, dd_out,
            wbuf, wt, gw, grecv, rep, maskx, own, acc_h, part, xbuf, rbuf, sbuf, hbuf, sibp, sst, gbuf, pbuf, xt,
            rdx, ddx, ddr, bias, gbacc, gbrecv, msgs, smsg, lossx, lossf,
@@ -98,12 +98,19 @@
                                                loc_sem.at[len(loads)]))
     my_cols = pl.ds(pl.multiple_of(c * v_loc, v_loc), v_loc)
     sib_cols = pl.ds(pl.multiple_of(o * v_loc, v_loc), v_loc)
-    load_m = pltpu.make_async_copy(msg_ref, msgs.at[me], loc_sem.at[len(loads)])
-    load_w = pltpu.make_async_copy(w_ref, wbuf.at[:, my_cols], loc_sem.at[len(loads) + 1])
-    load_b = pltpu.make_async_copy(b_ref, bias.at[:, my_cols], loc_sem.at[len(loads) + 2])
-    for cp in loads + [load_m, load_w, load_b]:
+    load_w = pltpu.make_async_copy(w_ref, wbuf.at[:, my_cols], loc_sem.at[len(loads)])
+    load_b = pltpu.make_async_copy(b_ref, bias.at[:, my_cols], loc_sem.at[len(loads) + 1])
+    for cp in loads + [load_w, load_b]:
         cp.start()
     xbuf[...] = jnp.zeros_like(xbuf)
+
+    where = jnp.concatenate([pos_ref[...], jnp.zeros((1, LANE - q_rows), jnp.int32)], axis=1)
+    for cc in WAYS:
+        tokens = jnp.concatenate([qm_ref[r:r + 1, :] for r in range(cc, q_rows, PAIR)]
+                                 + [dm_ref[r:r + 1, :] for r in range(cc, d_rows, PAIR)], axis=1)
+        for r in range(tokens.shape[1] // LANE):
+            msgs[me, cc, r:r + 1, :] = tokens[:, r * LANE:(r + 1) * LANE].astype(F32)
+        msgs[me, cc, 3:4, :] = where.astype(F32)
 
     barrier = pltpu.get_barrier_semaphore()
     for d in others:
@@ -113,7 +120,7 @@
     def remote(src, dst, ss, rs, to):
         return pltpu.make_async_remote_copy(src, dst, ss, rs, device_id=to, device_id_type=MESH)
 
-    send_m = [remote(msg_ref, msgs.at[me], msg_send.at[k], msg_recv.at[k], d) for k, d in enumerate(others)]
+    send_m = [remote(msgs.at[me], msgs.at[me], msg_send.at[k], msg_recv.at[k], d) for k, d in enumerate(others)]
     for cp in send_m:
         cp.start()
     send_w = remote(w_ref, wbuf.at[:, my_cols], w_sem.at[0], w_sem.at[1], sib)
@@ -251,7 +258,6 @@
     def _(i):
         gw[pl.ds(pl.multiple_of(i * BIG, BIG), BIG), :] = jnp.zeros((BIG, v_chip), F32)
 
-    load_m.wait()
     for cp in send_m:
         cp.wait()
 
@@ -313,9 +319,16 @@
         inject(KF, j)
         take_own(KF, j - KF[0])
         arrive(KF, j - KF[0], 0, 0)
-        fwd_group(j, b, 0, 0, cut(6))
+        near_left = j < n_unit + max(KF[s] for s in near)
+
+        @pl.when(near_left)
+        def _():
+            fwd_group(j, b, 0, 0, cut(6))
         relay(KF, j - 2, 3)
-        fwd_group(j, b, 0, cut(6), n_chunk)
+
+        @pl.when(near_left)
+        def _():
+            fwd_group(j, b, 0, cut(6), n_chunk)
         release(KF, j, near)
         relay(KF, j - 1, 2)
         relay(KF, j - 3, 4)
@@ -347,9 +360,9 @@
     q0 = PAD // per_row
     d0 = q0 + n_qpage
 
-    @pl.loop(0, n_chunk)
+    @pl.loop(0, v_chip // CB)
     def _(k):
-        at = pl.ds(pl.multiple_of(k * CH, CH), CH)
+        at = pl.ds(pl.multiple_of(k * CB, CB), CB)
         for r in range(d_rows // PAIR):
             rdx[c, r * n_group:(r + 1) * n_group, at] = sum(rep[d0 + r * pieces + i, :, at] for i in range(pieces))
         q_sum = sum(rep[q0 + i, :, at] for i in range(n_qpage))
@@ -373,18 +386,18 @@
         return jnp.sum(d_reps(at), axis=0, keepdims=True) * (1.0 / d_total)
 
     def lanes(v):
-        return sum(v[:, t * LANE:(t + 1) * LANE] for t in range(CH // LANE))
+        return sum(v[:, t * LANE:(t + 1) * LANE] for t in range(CB // LANE))
 
     def score_chunk(k, carry):
         s_acc, rq, rd = carry
-        at = pl.ds(pl.multiple_of(k * CH, CH), CH)
-        q_rep = rep[q0:q0 + n_qpage, :, at].reshape(nq, CH)
+        at = pl.ds(pl.multiple_of(k * CB, CB), CB)
+        q_rep = rep[q0:q0 + n_qpage, :, at].reshape(nq, CB)
         s_acc = s_acc + lax.dot_general(d_reps(at), q_rep, (((1,), (1,)), ((), ())), precision=HIGHEST,
                                         preferred_element_type=F32)
         qm, dm = q_mean_of(at), d_mean_of(at)
         return s_acc, rq + lanes(qm * qm), rd + lanes(dm * dm)
 
-    score, reg_q, reg_d = lax.fori_loop(0, n_chunk, score_chunk,
+    score, reg_q, reg_d = lax.fori_loop(0, v_chip // CB, score_chunk,
                                         (jnp.zeros((PAIR * nd, nq), F32), jnp.zeros((1, LANE), F32), jnp.zeros((1, LANE), F32)))
 
     def turn(n):
@@ -436,10 +449,10 @@
     inject(KB, ZERO + 1, BWD)
     relay(KB, ZERO, 2, BWD)
 
-    @pl.loop(0, n_chunk)
+    @pl.loop(0, v_chip // CB)
     def _(k):
-        at = pl.ds(pl.multiple_of(k * CH, CH), CH)
-        q_rep = rep[q0:q0 + n_qpage, :, at].reshape(nq, CH)
+        at = pl.ds(pl.multiple_of(k * CB, CB), CB)
+        q_rep = rep[q0:q0 + n_qpage, :, at].reshape(nq, CB)
         dp = exact(gt, q_rep)
         ddx[0, :, at] = dp[0:nd]
         ddx[1, :, at] = dp[nd:PAIR * nd]
@@ -447,11 +460,11 @@
     send_dd = to_sib(ddx.at[o], ddr, 2)
     send_dd.start()
 
-    @pl.loop(0, n_chunk)
+    @pl.loop(0, v_chip // CB)
     def _(k):
-        at = pl.ds(pl.multiple_of(k * CH, CH), CH)
+        at = pl.ds(pl.multiple_of(k * CB, CB), CB)
         gq = exact(g, d_reps(at)) + q_mean_of(at) * (2.0 * lam_q / q_total)
-        rep[q0:q0 + n_qpage, :, at] = gq.reshape(n_qpage, n_group, CH)
+        rep[q0:q0 + n_qpage, :, at] = gq.reshape(n_qpage, n_group, CB)
 
     send_l.wait()
     reg = (jnp.sum(total[PAIR * nd:PAIR * nd + 1, :], axis=1, keepdims=True) * lam_q
@@ -469,37 +482,40 @@
     relay(KB, ZERO, 3, BWD)
     send_dd.wait()
 
-    @pl.loop(0, n_chunk)
+    @pl.loop(0, v_chip // CB)
     def _(k):
-        at = pl.ds(pl.multiple_of(k * CH, CH), CH)
+        at = pl.ds(pl.multiple_of(k * CB, CB), CB)
         gd = ddx[c, :, at] + ddr[:, at] + d_mean_of(at) * (2.0 * lam_d / d_total)
         for r in range(d_rows // PAIR):
             for i in range(pieces):
                 rep[d0 + r * pieces + i, :, at] = gd[r * n_group:(r + 1) * n_group]
 
-    def bwd_chunk(j, b, page, k):
+    def bwd_chunk(j, b, page, k, slots=ORDER, weights=BWD):
+        at0 = pos[slots[0]] * br
+        some = slice(at0, at0 + len(slots) * br)
         cols = pl.ds(pl.multiple_of(k * CB, CB), CB)
-        logits = jnp.dot(xbuf[b], wbuf[:, cols], preferred_element_type=F32)
+        logits = jnp.dot(xbuf[b, some], wbuf[:, cols], preferred_element_type=F32)
         low = []
         for t in range(CB // LANE):
             at = pl.ds(pl.multiple_of(k * CB + t * LANE, LANE), LANE)
             zt = logits[:, t * LANE:(t + 1) * LANE] + bias[:, at]
             grad = jnp.concatenate([jnp.broadcast_to(rep[page[s], PAIR * s + u:PAIR * s + u + 1, at], (UT, LANE))
-                                    for s in ORDER for u in WAYS], axis=0)
-            gz = jnp.where(zt > 0.0, grad * mask_rows(j, KB, ORDER) / (1.0 + jnp.maximum(zt, 0.0)), 0.0)
-            gbacc[:, at] = gbacc[:, at] + jnp.sum(gz.reshape(rows // SUB, SUB, LANE), axis=0)
+                                    for s in slots for u in WAYS], axis=0)
+            gz = jnp.where(zt > 0.0, grad * mask_rows(j, KB, slots) / (1.0 + jnp.maximum(zt, 0.0)), 0.0)
+            gbacc[:, at] = gbacc[:, at] + jnp.sum(gz.reshape(-1, SUB, LANE), axis=0)
             low.append(gz.astype(BF16))
         low = jnp.concatenate(low, axis=1)
-        gbuf[:, cols] = low
-        gw[:, cols] = gw[:, cols] + jnp.dot(xt[...], low, preferred_element_type=F32)
-
-    def bwd_hidden(k0, k1):
+        gbuf[some, cols] = low
+        if weights:
+            gw[:, cols] = gw[:, cols] + jnp.dot(xt[...], low, preferred_element_type=F32)
+
+    def bwd_hidden(k0, k1, some=slice(None)):
         wide = hid // 4
 
         @functools.partial(lax.fori_loop, k0, k1, init_val=None, unroll=UNROLL)
         def _(k, _):
             cols = pl.ds(pl.multiple_of(k * wide, wide), wide)
-            pbuf[:, cols] = jnp.dot(gbuf[...], wt[:, cols], preferred_element_type=F32).astype(BF16)
+            pbuf[some, cols] = jnp.dot(gbuf[some, :], wt[:, cols], preferred_element_type=F32).astype(BF16)
 
     def deep(n):
         return lax.rem(n + BIG, DEEP)
@@ -607,6 +623,7 @@
                 pl.semaphore_signal(sp_cred, device_id=sib, device_id_type=MESH)
 
     last = n_unit + KB[MAXD]
+    assert all(n_unit + KB[s] < last for s in near)
 
     def part_b(eighths):
         return v_chip // CB * eighths // SUB
@@ -615,7 +632,7 @@
         for way in WAYS:
             rs_event(n, way, dist)
 
-    @pl.loop(1, last)
+    @pl.loop(1, last - 1)
     def _(j):
         b = par(j)
         page = pages(j, KB)
@@ -660,6 +677,35 @@
         pair_send(j - 1)
         pair_take(j - 2)
 
+    j = ZERO + last - 1
+    b = par(j)
+    page = pages(j, KB)
+    some = slice(half, rows)
+    relay(KB, j - 2, 4)
+    rs_both(j - 3, 4)
+    rs_both(j - 5, 1)
+
+    @functools.partial(lax.fori_loop, 0, v_chip // CB, init_val=None, unroll=UNROLL)
+    def _(k, _):
+        bwd_chunk(j, b, page, k, far, False)
+    rs_both(j - 4, 2)
+    bwd_hidden(0, 4, some)
+    for s in far:
+        if s != MAXD:
+            part[s, deep(j - KB[s])] = pbuf[block(s), :]
+    rs_both(j + 1 - 3, 4)
+    rs_both(j - 3, 3)
+    release(KB, j, ORDER)
+    pair_send(j - 1)
+    pair_take(j - 2)
+    rs_home(j - 5)
+    xt[:, some] = xbuf[b, some].T
+
+    @functools.partial(lax.fori_loop, 0, v_chip // CB, init_val=None, unroll=UNROLL)
+    def _(k, _):
+        cols = pl.ds(pl.multiple_of(k * CB, CB), CB)
+        gw[:, cols] = gw[:, cols] + jnp.dot(xt[:, some], gbuf[some, cols], preferred_element_type=F32)
+
     n_part = gx_send.shape[0] - 1
     step = v_loc // n_part
     send_g = []
@@ -692,7 +738,8 @@
     n_load = len(loads)
     for j in range(last, n_unit + 5):
         n = ZERO + j
-        rs_both(n - 3, 4)
+        if j > last:
+            rs_both(n - 3, 4)
         rs_both(n - 5, 1)
         if j > last:
             add_part()
@@ -753,12 +800,6 @@
         n_unit = n_page * per_row
         rows = nz * PAIR * UT
         nd, nq = d_rows // PAIR * n_group, q_rows // PAIR * n_group
-        by_core = jnp.concatenate([jnp.swapaxes(q_mask.reshape(q_rows // PAIR, 2, q_len), 0, 1).reshape(2, -1),
-                                   jnp.swapaxes(d_mask.reshape(d_rows // PAIR, 2, d_len), 0, 1).reshape(2, -1)], axis=1)
-        by_core = by_core.astype(F32).reshape(2, -1, LANE)
-        by_core = jnp.pad(by_core, ((0, 0), (0, 3 - by_core.shape[1]), (0, 0)))
-        where = jnp.pad(positive.astype(F32), (0, LANE - q_rows)).reshape(1, 1, LANE)
-        msg = jnp.concatenate([by_core, jnp.broadcast_to(where, (2, 1, LANE))], axis=1)
         s_rows = -(-(PAIR * nd + 2) // SUB) * SUB
         n_part = 4 if v_loc >= 512 else 2
         n_load = PAIR * (1 + d_rows // PAIR)
@@ -806,17 +847,18 @@
             dma((PAIR, MAXD, 2)), dma((PAIR, nz, 2)), reg((PAIR, MAXD)), dma((PAIR, 2)), reg((PAIR, 2)), dma, reg,
             dma((PAIR, MAXD)), dma((PAIR, MAXD - 1, DEEP)), reg((PAIR, MAXD)), dma((PAIR, 2)), dma((PAIR, 2, DEEP)), reg((PAIR, 2)),
             dma((PAIR,)), dma((PAIR,)), reg,
-            dma((n_load + 3,)), dma((PAIR,)), dma((PAIR,)), dma((n_group - 1,)), dma((n_group - 1,)), dma((nz,)), dma((nz,)),
+            dma((n_load + PAIR,)), dma((PAIR,)), dma((PAIR,)), dma((n_group - 1,)), dma((n_group - 1,)), dma((nz,)), dma((nz,)),
             dma((3, 2)), dma((n_part + 1,)), dma((n_part + 1,)), reg, dma((nz,)), dma, dma((n_load + n_part,)),
         ]
         loss, gw, gb, dq, dd = pl.pallas_call(
             functools.partial(kernel, n_group, q_rows, q_len, d_rows, d_len),
             out_shape=out_shape,
-            in_specs=[anym] * 5,
+            in_specs=[anym] * 4 + [vm] * 3,
             out_specs=(vm, anym, vm, anym, anym),
             scratch_shapes=scratch,
             compiler_params=pltpu.CompilerParams(collective_id=0, has_side_effects=True, vmem_limit_bytes=67043328),
-        )(q_hidden.reshape(q_shape), d_hidden.reshape(d_shape), w_head, b_head.reshape(1, v_loc), msg)
+        )(q_hidden.reshape(q_shape), d_hidden.reshape(d_shape), w_head, b_head.reshape(1, v_loc),
+          q_mask, d_mask, positive.reshape(1, q_rows))
         return (loss.reshape(1), gw, gb.reshape(v_loc), dq.reshape(q_hidden.shape), dd.reshape(d_hidden.shape))
 
     return jax.shard_map(local_step, mesh=mesh,

time: 473 us -> 467 us (0.987)
  no operation moved by 1% of the time
where the time goes in v4:
time: 467 us
  Pallas kernels  457 us (98%)
  local copies, waits for them, and re-layouts  7.28 us (2%)
    pallas_call x1, Pallas kernels, local_step(): pl.pallas_call(functools.partial(kernel, n_group, q_rows, q_len, d_rows,...  457 us

profile of v4, /device:TPU:21, one launch (start us, length us, event | category | flops | bytes accessed | tf_op | source)
XLA Modules:
  0.0 467.0 jit_solution(3989150160931132298)
XLA Ops:
  0.6 457.3 %shard_map.110 = (f32[1,1]{1,0:T(1,128)}, bf16[1024,2048]{1,0:T(8,128)(2,1)}, f32[1,2048]{1,0:T(1,128)}, bf16[8,2,32,1024]{3,2,1,0:T(8,128)(2,1)}, bf16[1,2,4,32,1024]{4,3,2,1,0:T(8,128)(2,1)}) custom-call(bf16[8,2,32,1024]{3,2,1,0:T(8,128)(2,1)} %bitcast.8, bf16[1,2,4,32,1024]{4,3,2,1,0:T(8,128)(2,1)} %bitcast.10, bf16[1024,2048]{1,0:T(8,128)(2,1)} %w_ref.1, ...), custom_call_target="tpu_custom_call" | custom-call | tf_op jit(solution)/shard_map/pallas_call | solution.py:853
  458.5 0.0 copy-start.2
  458.6 0.0 copy-start
  458.6 0.0 copy-start.1
  458.6 4.9 %copy.18 = bf16[1024,2048]{1,0:T(8,128)(2,1)} copy(bf16[1024,2048]{1,0:T(8,128)(2,1)} %get-tuple-element.21) | data formatting | bytes 8388608
  463.5 0.0 copy-done.2
  463.5 0.6 copy.19
  464.1 0.0 copy-done
  464.1 1.0 copy.20
  465.1 0.0 copy-done.1
  465.1 0.8 copy.21
Async XLA Ops:
  458.5 4.9 %copy-start.2 = (f32[1,2048]{1,0:T(1,128)S(1)}, f32[1,2048]{1,0:T(1,128)}, u32[]{:S(2)}) copy-start(f32[1,2048]{1,0:T(1,128)} %get-tuple-element.12) | copy-start | bytes 24580
  458.6 5.5 %copy-start = (bf16[8,2,32,1024]{3,2,1,0:T(8,128)(2,1)S(1)}, bf16[8,2,32,1024]{3,2,1,0:T(8,128)(2,1)}, u32[]{:S(2)}) copy-start(bf16[8,2,32,1024]{3,2,1,0:T(8,128)(2,1)} %get-tuple-element.13) | copy-start | bytes 3145732
  458.6 6.5 %copy-start.1 = (bf16[1,2,4,32,1024]{4,3,2,1,0:T(8,128)(2,1)S(1)}, bf16[1,2,4,32,1024]{4,3,2,1,0:T(8,128)(2,1)}, u32[]{:S(2)}) copy-start(bf16[1,2,4,32,1024]{4,3,2,1,0:T(8,128)(2,1)} %get-tuple-element.14) | copy-start | bytes 1572868

commit v5 on v4

--- a/solution.py
+++ b/solution.py
@@ -21,6 +21,7 @@
 KB = (1, 1, 1, 2, 2, 2, 1, 1)
 LANE, SUB, PAIR, BIG = 128, 8, 2, 64
 DEEP = 4
+ROOM = 8
 WAYS = (0, 1)
 ORDER = (0, 1, 7, 2, 6, 3, 5, 4)
 PAD = 4
@@ -32,7 +33,7 @@
            wbuf, wt, gw, grecv, rep, maskx, own, acc_h, part, xbuf, rbuf, sbuf, hbuf, sibp, sst, gbuf, pbuf, xt,
            rdx, ddx, ddr, bias, gbacc, gbrecv, msgs, smsg, lossx, lossf,
            ag_send, ag_recv, ag_cred, inj_send, inj_cred, sib_send, sib_cred,
-           rs_send, rs_recv, rs_cred, h_send, h_recv, h_cred, sp_send, sp_recv, sp_cred,
+           rs_send, rs_recv, h_send, h_recv, sp_send, sp_recv,
            loc_sem, w_sem, bias_sem, msg_send, msg_recv, sm_send, sm_recv, pair_sem, gx_send, gx_recv, gx_cred,
            loss_send, loss_recv, out_sem):
     ZERO = jnp.int32(0)
@@ -130,31 +131,42 @@
     for cp in loads:
         cp.wait()
 
-    def carries(way, dist, n, stop=n_unit):
-        ok = (n >= 0) & (n < stop)
-        if dist == MAXD:
-            ok = ok & (par(n) == way)
-        return ok
-
-    def credits_before(k, way, dist, n, bwd):
-        later = n >= 3 - k[slot(way, dist) % nz]
-        if not bwd:
-            return [(later, 1)]
-        if dist < MAXD:
-            return [(n == 0, 2), (later, 1)]
-        return [(n < 2, 1), (later, 1)]
-
-    def wait_credit(sem, k, way, dist, n, bwd):
-        for cond, amount in credits_before(k, way, dist, n, bwd):
+    steady = []
+
+    def guard(cond):
+        return (lambda f: f()) if cond is None else pl.when(cond)
+
+    def exists(n):
+        return None if steady else (n >= 0) & (n < n_unit)
+
+    def choose(way, a, b):
+        return jnp.where(way == 0, a, b)
+
+    def wait_credits(sems, k, s, n, bwd):
+        if steady:
+            for sem in sems:
+                pl.semaphore_wait(sem)
+            return
+        counts = [(n >= 3 - k[s], 1)]
+        if bwd:
+            counts.append((n < 2, 1) if s == MAXD else (n == 0, 2))
+        for cond, amount in counts:
             @pl.when(cond)
             def _():
-                pl.semaphore_wait(sem, amount)
+                for sem in sems:
+                    pl.semaphore_wait(sem, amount)
 
     def hop_copy(k, n, way, dist):
         s, s0 = slot(way, dist), slot(way, dist - 1)
         return remote(xbuf.at[par(n + k[s0]), block(s0)], xbuf.at[par(n + k[s]), block(s)],
                       ag_send.at[way, dist - 1, par(n)], ag_recv.at[par(n + k[s]), s, 0], dev(ahead[way], c))
 
+    def last_hop(k, n):
+        way, s0 = par(n), MAXD - 1
+        here = pl.ds(pl.multiple_of(choose(way, pos[s0] * br, pos[nz - s0] * br), br), br)
+        return remote(xbuf.at[par(n + k[s0]), here], xbuf.at[par(n + k[MAXD]), block(MAXD)],
+                      ag_send.at[way, s0, par(n)], ag_recv.at[par(n + k[MAXD]), MAXD, 0], dev(choose(way, right, left), c))
+
     def inj_copy(k, n, way, cc, i):
         s = slot(way, 1)
         return remote(own.at[cc, n // per_row, unit_rows(n)], xbuf.at[par(n + k[s]), part_of_block(s, i)],
@@ -165,82 +177,80 @@
                       sib_send, ag_recv.at[par(n + k[0]), 0, 0], sib)
 
     def inject(k, n, bwd=False):
-        @pl.when((n >= 0) & (n < n_unit))
-        def _():
-            for cc in WAYS:
-                for way in WAYS:
-                    wait_credit(inj_cred.at[way, cc], k, way, 1, n, bwd)
-                    inj_copy(k, n, way, cc, c).start()
-            wait_credit(sib_cred, k, 0, 0, n, bwd)
+        @guard(exists(n))
+        def _():
+            both = [(way, cc) for cc in WAYS for way in WAYS]
+            wait_credits([inj_cred.at[way, cc] for way, cc in both] + [sib_cred], k, 0, n, bwd)
+            for way, cc in both:
+                inj_copy(k, n, way, cc, c).start()
             sib_copy(k, n).start()
 
     def injected(k, n):
-        @pl.when((n >= 0) & (n < n_unit))
+        @guard(exists(n))
         def _():
             for cc in WAYS:
                 for way in WAYS:
                     inj_copy(k, n, way, cc, c).wait_send()
             sib_copy(k, n).wait_send()
 
-    def arrive(k, n, way, dist):
-        @pl.when(carries(way, dist, n))
-        def _():
-            if dist == 0:
-                sib_copy(k, n).wait_recv()
-            elif dist == 1:
-                for i in WAYS:
-                    inj_copy(k, n, way, 0, i).wait_recv()
-            else:
-                hop_copy(k, n, way, dist).wait_recv()
-
-    def forward(k, n, way, dist, bwd=False):
-        @pl.when(carries(way, dist + 1, n))
-        def _():
-            wait_credit(ag_cred.at[way, dist], k, way, dist + 1, n, bwd)
-            hop_copy(k, n, way, dist + 1).start()
-
     def relay(k, n, dist, bwd=False):
-        for way in WAYS:
-            arrive(k, n, way, dist)
-            if dist < MAXD:
-                forward(k, n, way, dist, bwd)
-
-    def take_own(k, n):
-        @pl.when((n >= 0) & (n < n_unit))
+        @guard(exists(n))
+        def _():
+            if dist == MAXD:
+                last_hop(k, n).wait_recv()
+                return
+            for way in WAYS:
+                if dist == 1:
+                    for i in WAYS:
+                        inj_copy(k, n, way, 0, i).wait_recv()
+                else:
+                    hop_copy(k, n, way, dist).wait_recv()
+                if dist < MAXD - 1:
+                    wait_credits([ag_cred.at[way, dist]], k, slot(way, dist + 1), n, bwd)
+                    hop_copy(k, n, way, dist + 1).start()
+            if dist == MAXD - 1:
+                wait_credits([ag_cred.at[par(n), dist]], k, MAXD, n, bwd)
+                last_hop(k, n).start()
+
+    def own_chip(k, n):
+        @guard(exists(n))
         def _():
             xbuf[par(n + k[0]), part_of_block(0, c)] = own[c, n // per_row, unit_rows(n)]
-
-    def give_credit(way, dist, amount=1):
+            sib_copy(k, n).wait_recv()
+
+    def give_credit(s, way, amount=1):
+        dist = dist_of(s)
         if dist == 0:
             pl.semaphore_signal(sib_cred, inc=amount, device_id=sib, device_id_type=MESH)
         elif dist == 1:
             for i in WAYS:
                 pl.semaphore_signal(inj_cred.at[way, c], inc=amount, device_id=dev(behind[way], i), device_id_type=MESH)
+        elif dist < MAXD:
+            pl.semaphore_signal(ag_cred.at[way, dist - 1], inc=amount, device_id=dev(behind[way], c), device_id_type=MESH)
         else:
-            pl.semaphore_signal(ag_cred.at[way, dist - 1], inc=amount, device_id=dev(behind[way], c), device_id_type=MESH)
-
-    def lanes_of(s):
-        if s == 0:
-            return ((0, 0),)
-        if s == MAXD:
-            return ((0, MAXD), (1, MAXD))
-        return ((0, s),) if s < MAXD else ((1, nz - s),)
+            pl.semaphore_signal(ag_cred.at[way, dist - 1], inc=amount, device_id=dev(choose(way, left, right), c),
+                                device_id_type=MESH)
+
+    def way_of(s):
+        return 0 if s < MAXD else 1
 
     def release(k, j, slots):
         for s in slots:
-            for way, dist in lanes_of(s):
-                n = j - k[s]
-                if 1 <= dist < MAXD:
-                    @pl.when(carries(way, dist + 1, n))
-                    def _():
-                        hop_copy(k, n, way, dist + 1).wait_send()
+            n, dist = j - k[s], dist_of(s)
+            if 1 <= dist < MAXD - 1 or s == MAXD - 1:
+                @guard(exists(n))
+                def _():
+                    (last_hop(k, n) if s == MAXD - 1 else hop_copy(k, n, way_of(s), dist + 1)).wait_send()
         for s in slots:
-            for way, dist in lanes_of(s):
-                @pl.when(carries(way, dist, j - k[s] + 2))
-                def _():
-                    give_credit(way, dist)
+            n = j - k[s] + 2
+
+            @guard(exists(n))
+            def _():
+                give_credit(s, par(n) if s == MAXD else way_of(s))
 
     near, far = ORDER[:nz // PAIR], ORDER[nz // PAIR:]
+    for k in (KF, KB):
+        assert k[0] == k[1] == k[nz - 1] and k[MAXD - 1] == k[MAXD + 1] and {MAXD - 1, MAXD, MAXD + 1} <= set(far)
 
     inject(KF, ZERO)
 
@@ -317,8 +327,7 @@
         b = par(j)
         release_far(j - 1)
         inject(KF, j)
-        take_own(KF, j - KF[0])
-        arrive(KF, j - KF[0], 0, 0)
+        own_chip(KF, j - KF[0])
         near_left = j < n_unit + max(KF[s] for s in near)
 
         @pl.when(near_left)
@@ -346,8 +355,11 @@
     release_far(jnp.int32(fwd_end - 1))
 
     for s in range(nz):
-        for way, dist in lanes_of(s):
-            give_credit(way, dist, 2 if dist < MAXD else 1)
+        if s == MAXD:
+            for way in WAYS:
+                give_credit(s, way)
+        else:
+            give_credit(s, way_of(s), 2)
 
     q_total = q_rows * n_group
     d_total = d_rows * n_group
@@ -520,107 +532,87 @@
     def deep(n):
         return lax.rem(n + BIG, DEEP)
 
+    def room(n):
+        return lax.rem(n + BIG, ROOM)
+
     def rs_copy(n, way, dist):
-        return remote(sbuf.at[way, dist - 1], rbuf.at[way, dist - 2, deep(n)], rs_send.at[way, dist - 1],
-                      rs_recv.at[way, dist - 2, deep(n)], dev(behind[way], c))
+        to = behind[way] if isinstance(way, int) else choose(way, left, right)
+        return remote(sbuf.at[way, dist - 1], rbuf.at[way, dist - 2, room(n)], rs_send.at[way, dist - 1],
+                      rs_recv.at[way, dist - 2, room(n)], dev(to, c))
 
     def home_copy(n, way, cc, i):
-        return remote(sbuf.at[way, 0, pl.ds(i * UT, UT)], hbuf.at[way, cc, deep(n)], h_send.at[way, i],
-                      h_recv.at[way, cc, deep(n)], dev(behind[way], i))
+        return remote(sbuf.at[way, 0, pl.ds(i * UT, UT)], hbuf.at[way, cc, room(n)], h_send.at[way, i],
+                      h_recv.at[way, cc, room(n)], dev(behind[way], i))
 
     def pair_copy(n):
-        return remote(sst.at[par(n)], sibp.at[par(n)], sp_send.at[par(n)], sp_recv.at[par(n)], sib)
-
-    def rs_sent(n, way, dist):
-        @pl.when(carries(way, dist, n))
-        def _():
-            if dist == 1:
-                for i in WAYS:
-                    home_copy(n, way, c, i).wait_send()
+        return remote(sst.at[par(n)], sibp.at[deep(n)], sp_send.at[par(n)], sp_recv.at[deep(n)], sib)
+
+    def rs_sent(n, dist):
+        @guard(exists(n))
+        def _():
+            if dist == MAXD:
+                rs_copy(n, par(n), dist).wait_send()
+                return
+            for way in WAYS:
+                if dist == 1:
+                    for i in WAYS:
+                        home_copy(n, way, c, i).wait_send()
+                else:
+                    rs_copy(n, way, dist).wait_send()
+
+    def rs_both(n, dist):
+        rs_sent(n - (2 if dist == MAXD else 1), dist)
+
+        def joined(way, mine):
+            rs_copy(n, way, dist + 1).wait_recv()
+            sbuf[way, dist - 1] = (mine.astype(F32) + rbuf[way, dist - 1, room(n)].astype(F32)).astype(BF16)
+
+        @guard(exists(n))
+        def _():
+            if dist == MAXD:
+                sbuf[par(n), dist - 1] = pbuf[block(MAXD), :]
+                rs_copy(n, par(n), dist).start()
+            elif dist == MAXD - 1:
+                way = par(n)
+                sbuf[1 - way, dist - 1] = part[choose(way, nz - dist, dist), deep(n)]
+                rs_copy(n, 1 - way, dist).start()
+                joined(way, part[choose(way, dist, nz - dist), deep(n)])
+                rs_copy(n, way, dist).start()
             else:
-                rs_copy(n, way, dist).wait_send()
-
-    def rs_go(n, way, dist):
-        @pl.when(n >= DEEP)
-        def _():
-            if dist == 1:
-                for i in WAYS:
-                    pl.semaphore_wait(h_cred.at[way, i])
-            else:
-                pl.semaphore_wait(rs_cred.at[way, dist - 1])
-        if dist == 1:
-            for i in WAYS:
-                home_copy(n, way, c, i).start()
-        else:
-            rs_copy(n, way, dist).start()
-
-    def rs_event(n, way, dist):
-        s = slot(way, dist)
-        rs_sent(n - (2 if dist == MAXD else 1), way, dist)
-        mine = (lambda: pbuf[block(s), :]) if dist == MAXD else (lambda: part[s, deep(n)])
-        incoming = carries(way, dist + 1, n) if dist + 1 <= MAXD else None
-        if dist == MAXD:
-            alone, joined = carries(way, dist, n), None
-        elif dist + 1 == MAXD:
-            alone, joined = carries(way, dist, n) & (par(n) != way), incoming
-        else:
-            alone, joined = None, incoming
-        if alone is not None:
-            @pl.when(alone)
-            def _():
-                sbuf[way, dist - 1] = mine()
-                rs_go(n, way, dist)
-        if joined is not None:
-            @pl.when(joined)
-            def _():
-                rs_copy(n, way, dist + 1).wait_recv()
-                got = rbuf[way, dist - 1, deep(n)]
-                sbuf[way, dist - 1] = (mine().astype(F32) + got.astype(F32)).astype(BF16)
-
-                @pl.when(n + DEEP < n_unit)
-                def _():
-                    pl.semaphore_signal(rs_cred.at[way, dist], device_id=dev(ahead[way], c), device_id_type=MESH)
-                rs_go(n, way, dist)
+                for way in WAYS:
+                    joined(way, part[slot(way, dist), deep(n)])
+                    if dist == 1:
+                        for i in WAYS:
+                            home_copy(n, way, c, i).start()
+                    else:
+                        rs_copy(n, way, dist).start()
 
     def rs_home(n):
-        @pl.when((n >= 0) & (n < n_unit))
+        @guard(exists(n))
         def _():
             for cc in WAYS:
                 for way in WAYS:
                     home_copy(n, way, cc, 0).wait_recv()
                 at = unit_rows(n)
-                acc_h[cc, n // per_row, at] = (acc_h[cc, n // per_row, at].astype(F32) + hbuf[0, cc, deep(n)].astype(F32)
-                                               + hbuf[1, cc, deep(n)].astype(F32)).astype(BF16)
-
-                @pl.when(n + DEEP < n_unit)
-                def _():
-                    for way in WAYS:
-                        pl.semaphore_signal(h_cred.at[way, c], device_id=dev(ahead[way], cc), device_id_type=MESH)
+                acc_h[cc, n // per_row, at] = (acc_h[cc, n // per_row, at].astype(F32) + hbuf[0, cc, room(n)].astype(F32)
+                                               + hbuf[1, cc, room(n)].astype(F32)).astype(BF16)
 
     def pair_send(n):
-        @pl.when((n >= 2) & (n < n_unit + 2))
+        @guard(exists(n - 2))
         def _():
             pair_copy(n - 2).wait_send()
 
-        @pl.when((n >= 0) & (n < n_unit))
+        @guard(exists(n))
         def _():
             sst[par(n)] = pbuf[part_of_block(0, o), :]
-
-            @pl.when(n >= 2)
-            def _():
-                pl.semaphore_wait(sp_cred)
             pair_copy(n).start()
             acc_h[c, n // per_row, unit_rows(n)] = pbuf[part_of_block(0, c), :]
 
     def pair_take(n):
-        @pl.when((n >= 0) & (n < n_unit))
+        @guard(exists(n))
         def _():
             pair_copy(n).wait_recv()
-            acc_h[o, n // per_row, unit_rows(n)] = sibp[par(n)]
-
-            @pl.when(n + 2 < n_unit)
-            def _():
-                pl.semaphore_signal(sp_cred, device_id=sib, device_id_type=MESH)
+            acc_h[o, n // per_row, unit_rows(n)] = sibp[deep(n)]
 
     last = n_unit + KB[MAXD]
     assert all(n_unit + KB[s] < last for s in near)
@@ -628,14 +620,10 @@
     def part_b(eighths):
         return v_chip // CB * eighths // SUB
 
-    def rs_both(n, dist):
-        for way in WAYS:
-            rs_event(n, way, dist)
-
-    @pl.loop(1, last - 1)
-    def _(j):
+    def bwd_step(j):
         b = par(j)
         page = pages(j, KB)
+        late = None if steady else j >= 2
 
         def weights(k0, k1):
             @functools.partial(lax.fori_loop, k0, k1, init_val=None, unroll=UNROLL)
@@ -643,20 +631,19 @@
                 bwd_chunk(j, b, page, k)
 
         relay(KB, j - 2, 4)
-        take_own(KB, j - 1)
-        arrive(KB, j - 1, 0, 0)
+        own_chip(KB, j - 1)
         rs_both(j - 3, 4)
         rs_both(j - 5, 1)
         xt[...] = xbuf[b].T
         weights(0, part_b(4))
 
-        @pl.when(j >= 2)
+        @guard(late)
         def _():
             relay(KB, j, 1, BWD)
         rs_both(j - 4, 2)
         weights(part_b(4), part_b(6))
 
-        @pl.when(j >= 2)
+        @guard(late)
         def _():
             relay(KB, j - 1, 3, BWD)
         weights(part_b(6), v_chip // CB)
@@ -664,7 +651,7 @@
         rs_both(j - 3, 3)
         bwd_hidden(0, 3)
 
-        @pl.when(j >= 2)
+        @guard(late)
         def _():
             injected(KB, j)
         inject(KB, j + 1, BWD)
@@ -676,6 +663,20 @@
                 part[s, deep(j - KB[s])] = pbuf[block(s), :]
         pair_send(j - 1)
         pair_take(j - 2)
+
+    @pl.loop(1, last - 1)
+    def _(j):
+        middle = (j >= 6) & (j < n_unit - 1)
+
+        @pl.when(middle)
+        def _():
+            steady.append(BWD)
+            bwd_step(j)
+            steady.pop()
+
+        @pl.when(jnp.logical_not(middle))
+        def _():
+            bwd_step(j)
 
     j = ZERO + last - 1
     b = par(j)
@@ -749,8 +750,7 @@
         if j == last:
             add_part()
         rs_home(n - 5)
-    for way in WAYS:
-        rs_sent(jnp.int32(n_unit - 1), way, 1)
+    rs_sent(jnp.int32(n_unit - 1), 1)
 
     outs = []
     for cc in WAYS:
@@ -826,10 +826,10 @@
             pltpu.VMEM((PAIR, n_page, q_len, hid), BF16),
             pltpu.VMEM((nz, DEEP, PAIR * UT, hid), BF16),
             pltpu.VMEM((PAIR, rows, hid), BF16),
-            pltpu.VMEM((PAIR, MAXD - 1, DEEP, PAIR * UT, hid), BF16),
+            pltpu.VMEM((PAIR, MAXD - 1, ROOM, PAIR * UT, hid), BF16),
             pltpu.VMEM((PAIR, MAXD, PAIR * UT, hid), BF16),
-            pltpu.VMEM((PAIR, 2, DEEP, UT, hid), BF16),
-            pltpu.VMEM((PAIR, UT, hid), BF16),
+            pltpu.VMEM((PAIR, 2, ROOM, UT, hid), BF16),
+            pltpu.VMEM((DEEP, UT, hid), BF16),
             pltpu.VMEM((PAIR, UT, hid), BF16),
             pltpu.VMEM((rows, v_chip), BF16),
             pltpu.VMEM((rows, hid), BF16),
@@ -845,8 +845,8 @@
             pltpu.VMEM((PAIR, SUB, LANE), F32),
             pltpu.VMEM((PAIR, SUB, LANE), F32),
             dma((PAIR, MAXD, 2)), dma((PAIR, nz, 2)), reg((PAIR, MAXD)), dma((PAIR, 2)), reg((PAIR, 2)), dma, reg,
-            dma((PAIR, MAXD)), dma((PAIR, MAXD - 1, DEEP)), reg((PAIR, MAXD)), dma((PAIR, 2)), dma((PAIR, 2, DEEP)), reg((PAIR, 2)),
-            dma((PAIR,)), dma((PAIR,)), reg,
+            dma((PAIR, MAXD)), dma((PAIR, MAXD - 1, ROOM)), dma((PAIR, 2)), dma((PAIR, 2, ROOM)),
+            dma((PAIR,)), dma((DEEP,)),
             dma((n_load + PAIR,)), dma((PAIR,)), dma((PAIR,)), dma((n_group - 1,)), dma((n_group - 1,)), dma((nz,)), dma((nz,)),
             dma((3, 2)), dma((n_part + 1,)), dma((n_part + 1,)), reg, dma((nz,)), dma, dma((n_load + n_part,)),
         ]

time: 467 us -> 460 us (0.985)
  Pallas kernels: 457 us -> 450 us
    pallas_call x1, Pallas kernels: 457 us -> 450 us  [local_step(): pl.pallas_call(functools.partial(kernel, n_group, q_rows, q_len, d_rows,...]
where the time goes in v5:
time: 460 us
  Pallas kernels  450 us (98%)
  local copies, waits for them, and re-layouts  7.28 us (2%)
    pallas_call x1, Pallas kernels, local_step(): pl.pallas_call(functools.partial(kernel, n_group, q_rows, q_len, d_rows,...  450 us

profile of v5, /device:TPU:21, one launch (start us, length us, event | category | flops | bytes accessed | tf_op | source)
XLA Modules:
  0.0 459.9 jit_solution(1450088934590040482)
XLA Ops:
  0.6 450.2 %shard_map.110 = (f32[1,1]{1,0:T(1,128)}, bf16[1024,2048]{1,0:T(8,128)(2,1)}, f32[1,2048]{1,0:T(1,128)}, bf16[8,2,32,1024]{3,2,1,0:T(8,128)(2,1)}, bf16[1,2,4,32,1024]{4,3,2,1,0:T(8,128)(2,1)}) custom-call(bf16[8,2,32,1024]{3,2,1,0:T(8,128)(2,1)} %bitcast.8, bf16[1,2,4,32,1024]{4,3,2,1,0:T(8,128)(2,1)} %bitcast.10, bf16[1024,2048]{1,0:T(8,128)(2,1)} %w_ref.1, ...), custom_call_target="tpu_custom_call" | custom-call | tf_op jit(solution)/shard_map/pallas_call | solution.py:853
  451.5 0.0 copy-start.2
  451.5 0.0 copy-start
  451.5 0.0 copy-start.1
  451.5 4.9 %copy.18 = bf16[1024,2048]{1,0:T(8,128)(2,1)} copy(bf16[1024,2048]{1,0:T(8,128)(2,1)} %get-tuple-element.21) | data formatting | bytes 8388608
  456.4 0.0 copy-done.2
  456.4 0.6 copy.19
  457.0 0.0 copy-done
  457.0 1.0 copy.20
  458.0 0.0 copy-done.1
  458.0 0.8 copy.21
Async XLA Ops:
  451.5 4.9 %copy-start.2 = (f32[1,2048]{1,0:T(1,128)S(1)}, f32[1,2048]{1,0:T(1,128)}, u32[]{:S(2)}) copy-start(f32[1,2048]{1,0:T(1,128)} %get-tuple-element.12) | copy-start | bytes 24580
  451.5 5.5 %copy-start = (bf16[8,2,32,1024]{3,2,1,0:T(8,128)(2,1)S(1)}, bf16[8,2,32,1024]{3,2,1,0:T(8,128)(2,1)}, u32[]{:S(2)}) copy-start(bf16[8,2,32,1024]{3,2,1,0:T(8,128)(2,1)} %get-tuple-element.13) | copy-start | bytes 3145732
  451.5 6.5 %copy-start.1 = (bf16[1,2,4,32,1024]{4,3,2,1,0:T(8,128)(2,1)S(1)}, bf16[1,2,4,32,1024]{4,3,2,1,0:T(8,128)(2,1)}, u32[]{:S(2)}) copy-start(bf16[1,2,4,32,1024]{4,3,2,1,0:T(8,128)(2,1)} %get-tuple-element.14) | copy-start | bytes 1572868

commit v6 on v5

--- a/solution.py
+++ b/solution.py
@@ -346,12 +346,6 @@
         fwd_group(j, b, 1, cut(4), n_chunk)
         injected(KF, j)
 
-        @pl.when(j <= v_chip // 256)
-        def _():
-            for u in WAYS:
-                at = pl.ds(pl.multiple_of((j - 1) * 256 + u * LANE, LANE), LANE)
-                wt[at, :] = wbuf[:, at].T
-
     release_far(jnp.int32(fwd_end - 1))
 
     for s in range(nz):
@@ -428,6 +422,11 @@
     send_s = [remote(smsg.at[0], smsg.at[t], sm_send.at[t], sm_recv.at[t], peers[t - 1]) for t in range(1, nz)]
     for cp in send_s:
         cp.start()
+
+    @pl.loop(0, v_chip // LANE)
+    def _(k):
+        at = pl.ds(pl.multiple_of(k * LANE, LANE), LANE)
+        wt[at, :] = wbuf[:, at].T
 
     pos_rows = jnp.concatenate([msgs[i, 0, 3:4, :] for i in range(n_group)], axis=0)
     spread = (lax.broadcasted_iota(jnp.int32, (LANE, nq), 0)
@@ -630,32 +629,36 @@
             def _(k, _):
                 bwd_chunk(j, b, page, k)
 
+        @guard(late)
+        def _():
+            relay(KB, j - 1, 2, BWD)
         relay(KB, j - 2, 4)
         own_chip(KB, j - 1)
+        xt[...] = xbuf[b].T
+        weights(0, part_b(2))
         rs_both(j - 3, 4)
         rs_both(j - 5, 1)
-        xt[...] = xbuf[b].T
-        weights(0, part_b(4))
+        weights(part_b(2), part_b(4))
 
         @guard(late)
         def _():
             relay(KB, j, 1, BWD)
+        weights(part_b(4), part_b(6))
+
+        @guard(late)
+        def _():
+            relay(KB, j - 1, 3, BWD)
         rs_both(j - 4, 2)
-        weights(part_b(4), part_b(6))
-
-        @guard(late)
-        def _():
-            relay(KB, j - 1, 3, BWD)
         weights(part_b(6), v_chip // CB)
         release(KB, j, ORDER)
         rs_both(j - 3, 3)
-        bwd_hidden(0, 3)
+        bwd_hidden(0, 2)
 
         @guard(late)
         def _():
             injected(KB, j)
         inject(KB, j + 1, BWD)
-        relay(KB, j, 2, BWD)
+        bwd_hidden(2, 3)
         rs_home(j - 5)
         bwd_hidden(3, 4)
         for s in range(1, nz):
@@ -780,6 +783,25 @@
     send_gb.wait_send()
     for cp in outs + w_outs:
         cp.wait()
+
+
+def settle(*refs):
+    n = len(refs) // 4
+    copies = []
+    for a, z, buf, sem in zip(*(refs[k * n:(k + 1) * n] for k in range(4))):
+        pieces = sem.shape[1]
+        size = a.shape[0] // pieces
+        for p in range(pieces):
+            at = pl.ds(p * size, size)
+            copies.append((pltpu.make_async_copy(a.at[at], buf.at[at], sem.at[0, p]),
+                           pltpu.make_async_copy(buf.at[at], z.at[at], sem.at[1, p])))
+    for cp, _ in copies:
+        cp.start()
+    for cp, back in copies:
+        cp.wait()
+        back.start()
+    for _, back in copies:
+        back.wait()
 
 
 def solution(mesh):
@@ -859,6 +881,15 @@
             compiler_params=pltpu.CompilerParams(collective_id=0, has_side_effects=True, vmem_limit_bytes=67043328),
         )(q_hidden.reshape(q_shape), d_hidden.reshape(d_shape), w_head, b_head.reshape(1, v_loc),
           q_mask, d_mask, positive.reshape(1, q_rows))
+        results = (gw, dq, dd, gb, loss)
+        gw, dq, dd, gb, loss = pl.pallas_call(
+            settle,
+            out_shape=[jax.ShapeDtypeStruct(a.shape, a.dtype) for a in results],
+            in_specs=[anym] * len(results),
+            out_specs=[anym] * len(results),
+            scratch_shapes=[pltpu.VMEM(a.shape, a.dtype) for a in results] + [dma((2, math.gcd(4, a.shape[0]))) for a in results],
+            compiler_params=pltpu.CompilerParams(vmem_limit_bytes=67043328),
+        )(*results)
         return (loss.reshape(1), gw, gb.reshape(v_loc), dq.reshape(q_hidden.shape), dd.reshape(d_hidden.shape))
 
     return jax.shard_map(local_step, mesh=mesh,

time: 460 us -> 465 us (1.011)
  Pallas kernels: 450 us -> 464 us
  local copies, waits for them, and re-layouts: 7.28 us -> 0 us
    pallas_call x1, Pallas kernels: 450 us -> 458 us  [local_step(): pl.pallas_call(functools.partial(kernel, n_group, q_rows, q_len, d_rows,...]
    unnamed x10 -> x0, local copies, waits for them, and re-layouts: 7.28 us -> none
    pallas_call x0 -> x1, Pallas kernels: none -> 5.3 us  [local_step(): pl.pallas_call(settle, out_shape=[jax.ShapeDtypeStruct(a.shape, a.dtype)...]
where the time goes in v6:
time: 465 us
  Pallas kernels  464 us (100%)
    pallas_call x1, Pallas kernels, local_step(): pl.pallas_call(functools.partial(kernel, n_group, q_rows, q_len, d_rows,...  458 us

profile of v6, /device:TPU:21, one launch (start us, length us, event | category | flops | bytes accessed | tf_op | source)
XLA Modules:
  0.0 464.5 jit_solution(16145507710087302003)
XLA Ops:
  0.6 458.4 %shard_map.110 = (f32[1,1]{1,0:T(1,128)}, bf16[1024,2048]{1,0:T(8,128)(2,1)}, f32[1,2048]{1,0:T(1,128)}, bf16[8,2,32,1024]{3,2,1,0:T(8,128)(2,1)}, bf16[1,2,4,32,1024]{4,3,2,1,0:T(8,128)(2,1)}) custom-call(bf16[8,2,32,1024]{3,2,1,0:T(8,128)(2,1)} %bitcast.8, bf16[1,2,4,32,1024]{4,3,2,1,0:T(8,128)(2,1)} %bitcast.9, bf16[1024,2048]{1,0:T(8,128)(2,1)} %w_ref.1, ...), custom_call_target="tpu_custom_call" | custom-call | tf_op jit(solution)/shard_map/pallas_call | solution.py:875
  459.0 5.3 %shard_map.111 = (bf16[1024,2048]{1,0:T(8,128)(2,1)}, bf16[8,2,32,1024]{3,2,1,0:T(8,128)(2,1)}, bf16[1,2,4,32,1024]{4,3,2,1,0:T(8,128)(2,1)}, f32[1,2048]{1,0:T(1,128)}, f32[1,1]{1,0:T(1,128)}) custom-call(bf16[1024,2048]{1,0:T(8,128)(2,1)} %get-tuple-element.15.refs_0_, bf16[8,2,32,1024]{3,2,1,0:T(8,128)(2,1)} %get-tuple-element.16.refs_1_, ...), custom_call_target="tpu_custom_call" | custom-call | tf_op jit(solution)/shard_map/pallas_call | solution.py:885

commit v7 on v6

--- a/solution.py
+++ b/solution.py
@@ -423,10 +423,11 @@
     for cp in send_s:
         cp.start()
 
-    @pl.loop(0, v_chip // LANE)
-    def _(k):
-        at = pl.ds(pl.multiple_of(k * LANE, LANE), LANE)
-        wt[at, :] = wbuf[:, at].T
+    def turn_head(first):
+        @pl.loop(0, v_chip // LANE // PAIR)
+        def _(k):
+            at = pl.ds(pl.multiple_of((first * (v_chip // LANE // PAIR) + k) * LANE, LANE), LANE)
+            wt[at, :] = wbuf[:, at].T
 
     pos_rows = jnp.concatenate([msgs[i, 0, 3:4, :] for i in range(n_group)], axis=0)
     spread = (lax.broadcasted_iota(jnp.int32, (LANE, nq), 0)
@@ -439,8 +440,10 @@
     doc = (ridx % n_group) * d_rows + PAIR * ((ridx % nd) // n_group) + ridx // nd
     target = (doc.astype(F32) == pos_row).astype(F32)
 
+    turn_head(0)
     relay(KB, ZERO, 1, BWD)
     injected(KB, ZERO)
+    turn_head(1)
     for cp in send_s:
         cp.wait()
     total = smsg[0]
@@ -629,36 +632,32 @@
             def _(k, _):
                 bwd_chunk(j, b, page, k)
 
-        @guard(late)
-        def _():
-            relay(KB, j - 1, 2, BWD)
         relay(KB, j - 2, 4)
         own_chip(KB, j - 1)
-        xt[...] = xbuf[b].T
-        weights(0, part_b(2))
         rs_both(j - 3, 4)
         rs_both(j - 5, 1)
-        weights(part_b(2), part_b(4))
+        xt[...] = xbuf[b].T
+        weights(0, part_b(4))
 
         @guard(late)
         def _():
             relay(KB, j, 1, BWD)
+        rs_both(j - 4, 2)
         weights(part_b(4), part_b(6))
 
         @guard(late)
         def _():
             relay(KB, j - 1, 3, BWD)
-        rs_both(j - 4, 2)
         weights(part_b(6), v_chip // CB)
         release(KB, j, ORDER)
         rs_both(j - 3, 3)
-        bwd_hidden(0, 2)
+        bwd_hidden(0, 3)
 
         @guard(late)
         def _():
             injected(KB, j)
         inject(KB, j + 1, BWD)
-        bwd_hidden(2, 3)
+        relay(KB, j, 2, BWD)
         rs_home(j - 5)
         bwd_hidden(3, 4)
         for s in range(1, nz):
@@ -744,14 +743,13 @@
         n = ZERO + j
         if j > last:
             rs_both(n - 3, 4)
+        if j == n_unit + 4:
+            add_part()
         rs_both(n - 5, 1)
-        if j > last:
-            add_part()
         rs_both(n - 4, 2)
         rs_both(n - 3, 3)
         pair_send(n - 1)
-        if j == last:
-            add_part()
+        add_part()
         rs_home(n - 5)
     rs_sent(jnp.int32(n_unit - 1), 1)
 

time: 465 us -> 455 us (0.978)
  Pallas kernels: 464 us -> 454 us
    pallas_call x1, Pallas kernels: 458 us -> 449 us  [local_step(): pl.pallas_call(functools.partial(kernel, n_group, q_rows, q_len, d_rows,...]
where the time goes in v7:
time: 455 us
  Pallas kernels  454 us (100%)
    pallas_call x1, Pallas kernels, local_step(): pl.pallas_call(functools.partial(kernel, n_group, q_rows, q_len, d_rows,...  449 us

profile of v7, /device:TPU:21, one launch (start us, length us, event | category | flops | bytes accessed | tf_op | source)
XLA Modules:
  0.0 454.9 jit_solution(10944417589171307598)
XLA Ops:
  0.6 448.8 %shard_map.110 = (f32[1,1]{1,0:T(1,128)}, bf16[1024,2048]{1,0:T(8,128)(2,1)}, f32[1,2048]{1,0:T(1,128)}, bf16[8,2,32,1024]{3,2,1,0:T(8,128)(2,1)}, bf16[1,2,4,32,1024]{4,3,2,1,0:T(8,128)(2,1)}) custom-call(bf16[8,2,32,1024]{3,2,1,0:T(8,128)(2,1)} %bitcast.8, bf16[1,2,4,32,1024]{4,3,2,1,0:T(8,128)(2,1)} %bitcast.9, bf16[1024,2048]{1,0:T(8,128)(2,1)} %w_ref.1, ...), custom_call_target="tpu_custom_call" | custom-call | tf_op jit(solution)/shard_map/pallas_call | solution.py:873
  449.4 5.3 %shard_map.111 = (bf16[1024,2048]{1,0:T(8,128)(2,1)}, bf16[8,2,32,1024]{3,2,1,0:T(8,128)(2,1)}, bf16[1,2,4,32,1024]{4,3,2,1,0:T(8,128)(2,1)}, f32[1,2048]{1,0:T(1,128)}, f32[1,1]{1,0:T(1,128)}) custom-call(bf16[1024,2048]{1,0:T(8,128)(2,1)} %get-tuple-element.15.refs_0_, bf16[8,2,32,1024]{3,2,1,0:T(8,128)(2,1)} %get-tuple-element.16.refs_1_, ...), custom_call_target="tpu_custom_call" | custom-call | tf_op jit(solution)/shard_map/pallas_call | solution.py:883

commit v8 on v7

--- a/solution.py
+++ b/solution.py
@@ -634,15 +634,14 @@
 
         relay(KB, j - 2, 4)
         own_chip(KB, j - 1)
+        xt[...] = xbuf[b].T
+        weights(0, part_b(4))
+
+        @guard(late)
+        def _():
+            relay(KB, j, 1, BWD)
         rs_both(j - 3, 4)
         rs_both(j - 5, 1)
-        xt[...] = xbuf[b].T
-        weights(0, part_b(4))
-
-        @guard(late)
-        def _():
-            relay(KB, j, 1, BWD)
-        rs_both(j - 4, 2)
         weights(part_b(4), part_b(6))
 
         @guard(late)
@@ -650,7 +649,7 @@
             relay(KB, j - 1, 3, BWD)
         weights(part_b(6), v_chip // CB)
         release(KB, j, ORDER)
-        rs_both(j - 3, 3)
+        rs_both(j - 4, 2)
         bwd_hidden(0, 3)
 
         @guard(late)
@@ -658,6 +657,7 @@
             injected(KB, j)
         inject(KB, j + 1, BWD)
         relay(KB, j, 2, BWD)
+        rs_both(j - 3, 3)
         rs_home(j - 5)
         bwd_hidden(3, 4)
         for s in range(1, nz):

time: 455 us -> 467 us (1.026)
  Pallas kernels: 454 us -> 466 us
    pallas_call x1, Pallas kernels: 449 us -> 461 us  [local_step(): pl.pallas_call(functools.partial(kernel, n_group, q_rows, q_len, d_rows,...]
where the time goes in v8:
time: 467 us
  Pallas kernels  466 us (100%)
    pallas_call x1, Pallas kernels, local_step(): pl.pallas_call(functools.partial(kernel, n_group, q_rows, q_len, d_rows,...  461 us

profile of v8, /device:TPU:21, one launch (start us, length us, event | category | flops | bytes accessed | tf_op | source)
XLA Modules:
  0.0 466.7 jit_solution(3594233149841362483)
XLA Ops:
  0.6 460.5 %shard_map.110 = (f32[1,1]{1,0:T(1,128)}, bf16[1024,2048]{1,0:T(8,128)(2,1)}, f32[1,2048]{1,0:T(1,128)}, bf16[8,2,32,1024]{3,2,1,0:T(8,128)(2,1)}, bf16[1,2,4,32,1024]{4,3,2,1,0:T(8,128)(2,1)}) custom-call(bf16[8,2,32,1024]{3,2,1,0:T(8,128)(2,1)} %bitcast.8, bf16[1,2,4,32,1024]{4,3,2,1,0:T(8,128)(2,1)} %bitcast.9, bf16[1024,2048]{1,0:T(8,128)(2,1)} %w_ref.1, ...), custom_call_target="tpu_custom_call" | custom-call | tf_op jit(solution)/shard_map/pallas_call | solution.py:873
  461.2 5.3 %shard_map.111 = (bf16[1024,2048]{1,0:T(8,128)(2,1)}, bf16[8,2,32,1024]{3,2,1,0:T(8,128)(2,1)}, bf16[1,2,4,32,1024]{4,3,2,1,0:T(8,128)(2,1)}, f32[1,2048]{1,0:T(1,128)}, f32[1,1]{1,0:T(1,128)}) custom-call(bf16[1024,2048]{1,0:T(8,128)(2,1)} %get-tuple-element.15.refs_0_, bf16[8,2,32,1024]{3,2,1,0:T(8,128)(2,1)} %get-tuple-element.16.refs_1_, ...), custom_call_target="tpu_custom_call" | custom-call | tf_op jit(solution)/shard_map/pallas_call | solution.py:883
